TPU v7x, 16 devices: a 4x2x1 block of a 4x4x8 slice. The times are simulated.
16 devices in a mesh: sys: 2 (over y, z), blk: 8 (over x, core).
Axes of the slice: x: 4, y: 2, z: 1, core: 2. Of those that a mesh axis runs over, the one named last changes fastest.
The devices are a block of a 4x4x8 slice.
Arguments:
- positions: float32 [16384, 256], P(('sys', 'blk')), parts along dimension 0
- velocity: float32 [16384, 256], P(('sys', 'blk')), parts along dimension 0
- charges: float32 [16384], P(('sys', 'blk')), parts along dimension 0
Outputs:
- output 1: float32 [16384, 256], P(('sys', 'blk')), parts along dimension 0
- output 2: float32 [2], P('sys'), parts along dimension 0
- output 3: float32 [16384, 256], P(('sys', 'blk')), parts along dimension 0
- output 4: float32 [16384, 256], P(('sys', 'blk')), parts along dimension 0
There are 2 independent parts. A program takes and returns all parts, laid end to end along the dimension named above; each array names one.
All inputs are finite; a program needn't handle non-finite values.
Results may differ from a plain program's by a relative error of at most 0.00326424.
Values are sent between devices in bfloat16 or wider.
A program may use at most 768 MiB of HBM per device.

v0:
```python
import jax
import jax.numpy as jnp
from jax import lax
from jax.sharding import PartitionSpec as P

STEP_SIZE = 0.5
ROW_TILE = 256


def block_pair(x_a, q_a, x_b, q_b, same_block, want_b):
    rows_a, feat_dim = x_a.shape
    rows_b = x_b.shape[0]
    ell_sq = 1.0 * feat_dim
    tile_rows = min(rows_a, ROW_TILE)
    sq_a = jnp.sum(jnp.square(x_a.astype(jnp.float32)), axis=1)
    sq_b = jnp.sum(jnp.square(x_b.astype(jnp.float32)), axis=1)
    col_ids = jnp.arange(rows_b)

    def tile_step(state_in, tile_idx):
        col_sum, back_sum, weight_total = state_in
        row_start = tile_idx * tile_rows
        x_tile = lax.dynamic_slice_in_dim(x_a, row_start, tile_rows, 0)
        q_tile = lax.dynamic_slice_in_dim(q_a, row_start, tile_rows, 0)
        sq_tile = lax.dynamic_slice_in_dim(sq_a, row_start, tile_rows, 0)
        gram_tile = jnp.einsum("id,jd->ij", x_tile, x_b, preferred_element_type=jnp.float32)
        dist_sq = jnp.maximum(sq_tile[:, None] + sq_b[None, :] - 2.0 * gram_tile, 0.0)
        weight = q_tile[:, None] * q_b[None, :] * jnp.exp(-dist_sq / (2.0 * ell_sq))
        if same_block:
            on_diag = (row_start + jnp.arange(tile_rows))[:, None] == col_ids[None, :]
            weight = jnp.where(on_diag, 0.0, weight)
        w_low = weight.astype(jnp.bfloat16)
        pull_sum = jnp.dot(w_low, x_b, preferred_element_type=jnp.float32)
        force_tile = jnp.sum(weight, axis=1)[:, None] * x_tile.astype(jnp.float32) - pull_sum
        if want_b:
            col_sum = col_sum + jnp.sum(weight, axis=0)
            back_sum = back_sum + jnp.einsum("ij,id->jd", w_low, x_tile, preferred_element_type=jnp.float32)
        return (col_sum, back_sum, weight_total + jnp.sum(weight)), force_tile

    if want_b:
        start_state = (jnp.zeros((rows_b,), jnp.float32), jnp.zeros((rows_b, feat_dim), jnp.float32), jnp.zeros((), jnp.float32))
    else:
        start_state = (jnp.zeros((), jnp.float32), jnp.zeros((), jnp.float32), jnp.zeros((), jnp.float32))
    end_state, force_tiles = lax.scan(tile_step, start_state, jnp.arange(rows_a // tile_rows))
    col_sum, back_sum, weight_total = end_state
    force_a = force_tiles.reshape(rows_a, feat_dim)
    react_b = col_sum[:, None] * x_b.astype(jnp.float32) - back_sum if want_b else None
    return force_a, react_b, weight_total


def paired_forces(positions, charges, blk_size):
    x_host = positions.astype(jnp.bfloat16)
    host_rows, feat_dim = x_host.shape
    my_index = lax.axis_index("blk")
    half_way = blk_size // 2
    odd_steps = (blk_size - 1) // 2
    next_perm = [(i, (i + 1) % blk_size) for i in range(blk_size)]
    home_perm = [(i, (i - half_way) % blk_size) for i in range(blk_size)]
    force_acc, _, self_sum = block_pair(x_host, charges, x_host, charges, True, False)
    energy_acc = 0.5 * self_sum
    react_acc = jnp.zeros((host_rows, feat_dim), jnp.float32)
    x_vis = x_host
    q_vis = charges
    if odd_steps >= 1:
        x_vis = lax.ppermute(x_host, "blk", next_perm)
        q_vis = lax.ppermute(charges, "blk", next_perm)
        force_new, react_acc, pair_sum = block_pair(x_host, charges, x_vis, q_vis, False, True)
        force_acc = force_acc + force_new
        energy_acc = energy_acc + pair_sum

        def pair_step(step_idx, state_in):
            force_run, energy_run, x_seen, q_seen, react_run = state_in
            x_seen = lax.ppermute(x_seen, "blk", next_perm)
            q_seen = lax.ppermute(q_seen, "blk", next_perm)
            react_run = lax.ppermute(react_run, "blk", next_perm)
            force_step, react_step, step_sum = block_pair(x_host, charges, x_seen, q_seen, False, True)
            return (force_run + force_step, energy_run + step_sum, x_seen, q_seen, react_run + react_step)

        force_acc, energy_acc, x_vis, q_vis, react_acc = lax.fori_loop(1, odd_steps, pair_step, (force_acc, energy_acc, x_vis, q_vis, react_acc))
    if blk_size % 2 == 0:
        x_vis = lax.ppermute(x_vis, "blk", next_perm)
        q_vis = lax.ppermute(q_vis, "blk", next_perm)
        if odd_steps >= 1:
            react_acc = lax.ppermute(react_acc, "blk", next_perm)
        mid_row = host_rows // 2
        is_lower = my_index < half_way
        x_a = jnp.where(is_lower, x_host[:mid_row], x_vis[mid_row:])
        q_a = jnp.where(is_lower, charges[:mid_row], q_vis[mid_row:])
        x_b = jnp.where(is_lower, x_vis, x_host)
        q_b = jnp.where(is_lower, q_vis, charges)
        force_half, react_full, pair_sum = block_pair(x_a, q_a, x_b, q_b, False, True)
        zero_half = jnp.zeros((mid_row, feat_dim), jnp.float32)
        force_acc = force_acc + jnp.where(is_lower, jnp.concatenate([force_half, zero_half]), react_full)
        react_acc = react_acc + jnp.where(is_lower, react_full, jnp.concatenate([zero_half, force_half]))
        energy_acc = energy_acc + pair_sum
    react_home = lax.ppermute(react_acc, "blk", home_perm)
    return (force_acc + react_home) / feat_dim, energy_acc


def solution(mesh):
    blk_size = mesh.shape["blk"]
    row_spec = P(("sys", "blk"), None)
    vec_spec = P(("sys", "blk"))

    def local_steps(positions, velocity, charges):
        force_zero, _ = paired_forces(positions, charges, blk_size)
        pos_one = positions + STEP_SIZE * velocity
        vel_one = velocity + STEP_SIZE * force_zero
        force_one, energy_local = paired_forces(pos_one, charges, blk_size)
        energy_one = lax.psum(energy_local, "blk").reshape(1)
        return force_one, energy_one, pos_one + STEP_SIZE * vel_one, vel_one + STEP_SIZE * force_one

    return jax.shard_map(local_steps, mesh=mesh, in_specs=(row_spec, row_spec, vec_spec), out_specs=(row_spec, P("sys"), row_spec, row_spec), check_vma=False)
```

profile of v0, /device:TPU:113, one launch (start us, length us, event | category | flops | bytes accessed | tf_op | source)
XLA Modules:
  0.0 409.4 jit_solution(4201781545672394857)
XLA Ops:
  0.6 3.1 multiply_reduce_fusion.3
  3.7 2.7 collective-permute-start.7
  8.2 26.1 %while.160 = (s32[]{:T(128)}, f32[]{:T(128)}, f32[4,256,256]{2,1,0:T(8,128)S(1)}, s32[4]{0:T(128)S(1)}, f32[1024]{0:T(1024)}, /*index=5*/f32[1024]{0:T(1024)S(1)...) while((s32[]{:T(128)}, f32[]{:T(128)}, ...), condition=%wide.region_4.5_spmd.clone, body=%wide.region_1.4_spmd.clone.sunk | while | flops 272039936 | bytes 2640587 | solution.py:43
  35.3 21.0 %while.161 = (s32[]{:T(128)}, f32[4,256,256]{2,1,0:T(8,128)S(1)}, s32[4]{0:T(128)S(1)}, f32[1024]{0:T(1024)}, f32[1024]{0:T(1024)S(1)}, /*index=5*/bf16[1024,256...) while((s32[]{:T(128)}, f32[4,256,256]{2,1,0:T(8,128)S(1)}, s32[4]{0:T(128)S(1)}, ...), condition=%wide.region_31.32_spmd.clone, body=%wide.region_29.31_spmd.clone.sunk | while | flops 271777792 | bytes 2640563 | solution.py:43
  58.7 32.1 %while.162 = (s32[]{:T(128)}, f32[1024]{0:T(1024)S(1)}, f32[1024,256]{1,0:T(8,128)S(1)}, f32[]{:T(128)}, f32[4,256,256]{2,1,0:T(8,128)S(1)}, /*index=5*/s32[4]{0...) while((s32[]{:T(128)}, f32[1024]{0:T(1024)S(1)}, ...), condition=%wide.region_10.11_spmd.clone, body=%wide.region_6.0_spmd.clone.sunk | while | flops 406520576 | bytes 5406978 | solution.py:43
  94.4 93.1 %while.157 = (s32[]{:T(128)}, f32[1024,256]{1,0:T(8,128)S(1)}, f32[]{:T(128)}, bf16[1024,256]{1,0:T(8,128)(2,1)}, f32[1024]{0:T(1024)S(1)}, /*index=5*/f32[1024,...) while((s32[]{:T(128)}, f32[1024,256]{1,0:T(8,128)S(1)}, ...), condition=%wide.region_19.20_spmd, body=%wide.region_11.19_spmd.sunk | while | flops 409402112 | bytes 20649136 | solution.py:78
  97.1 3.4 collective-permute-done.3
  100.8 34.2 %while.166 = (s32[]{:T(128)}, f32[1024]{0:T(1024)S(1)}, f32[1024,256]{1,0:T(8,128)S(1)}, f32[]{:T(128)}, f32[4,256,256]{2,1,0:T(8,128)}, /*index=5*/s32[4]{0:T(1...) while((s32[]{:T(128)}, f32[1024]{0:T(1024)S(1)}, ...), condition=%wide.region_18.18_spmd.clone, body=%wide.region_14.17_spmd.clone.sunk | while | flops 406520576 | bytes 5407486 | solution.py:43
  144.9 3.4 collective-permute-done.3
  148.6 34.2 %while.166 = (s32[]{:T(128)}, f32[1024]{0:T(1024)S(1)}, f32[1024,256]{1,0:T(8,128)S(1)}, f32[]{:T(128)}, f32[4,256,256]{2,1,0:T(8,128)}, /*index=5*/s32[4]{0:T(1...) while((s32[]{:T(128)}, f32[1024]{0:T(1024)S(1)}, ...), condition=%wide.region_18.18_spmd.clone, body=%wide.region_14.17_spmd.clone.sunk | while | flops 406520576 | bytes 5407486 | solution.py:43
  192.4 29.4 %while.164 = (s32[]{:T(128)}, f32[1024]{0:T(1024)S(1)}, f32[1024,256]{1,0:T(8,128)S(1)}, f32[4,256,256]{2,1,0:T(8,128)}, s32[4]{0:T(128)S(1)}, /*index=5*/f32[10...) while((s32[]{:T(128)}, f32[1024]{0:T(1024)S(1)}, ...), condition=%wide.region_36.37_spmd.clone, body=%wide.region_33.36_spmd.clone.sunk | while | flops 406258432 | bytes 5407462 | solution.py:43
  226.8 82.8 %while.159 = (s32[]{:T(128)}, f32[1024,256]{1,0:T(8,128)S(1)}, bf16[1024,256]{1,0:T(8,128)(2,1)}, f32[1024]{0:T(1024)S(1)}, f32[1024,256]{1,0:T(8,128)}, /*index...) while((s32[]{:T(128)}, f32[1024,256]{1,0:T(8,128)S(1)}, ...), condition=%wide.region_44.45_spmd, body=%wide.region_37.44_spmd.sunk | while | flops 409139968 | bytes 20649068 | solution.py:78
  230.0 4.3 %collective-permute-done = f32[1024]{0:T(1024)S(1)} collective-permute-done((f32[1024]{0:T(1024)S(1)}, f32[1024]{0:T(1024)S(1)}, u32[]{:S(2)}, u32[]{:S(2)}) %collective-permute-start) | collective-permute-done | bytes 4128 | tf_op jit(solution)/shard_map/while/body/eval_jaxpr/ppermute | solution.py:73
  234.6 28.4 %while.167 = (s32[]{:T(128)}, f32[1024]{0:T(1024)S(1)}, f32[1024,256]{1,0:T(8,128)S(1)}, f32[4,256,256]{2,1,0:T(8,128)}, s32[4]{0:T(128)S(1)}, /*index=5*/f32[10...) while((s32[]{:T(128)}, f32[1024]{0:T(1024)S(1)}, ...), condition=%wide.region_43.43_spmd.clone, body=%wide.region_40.42_spmd.clone.sunk | while | flops 406258432 | bytes 5407462 | solution.py:43
  267.7 2.5 collective-permute-start.1
  272.0 4.4 %collective-permute-done = f32[1024]{0:T(1024)S(1)} collective-permute-done((f32[1024]{0:T(1024)S(1)}, f32[1024]{0:T(1024)S(1)}, u32[]{:S(2)}, u32[]{:S(2)}) %collective-permute-start) | collective-permute-done | bytes 4128 | tf_op jit(solution)/shard_map/while/body/eval_jaxpr/ppermute | solution.py:73
  276.6 28.4 %while.167 = (s32[]{:T(128)}, f32[1024]{0:T(1024)S(1)}, f32[1024,256]{1,0:T(8,128)S(1)}, f32[4,256,256]{2,1,0:T(8,128)}, s32[4]{0:T(128)S(1)}, /*index=5*/f32[10...) while((s32[]{:T(128)}, f32[1024]{0:T(1024)S(1)}, ...), condition=%wide.region_43.43_spmd.clone, body=%wide.region_40.42_spmd.clone.sunk | while | flops 406258432 | bytes 5407462 | solution.py:43
  321.3 9.3 %while.163 = (s32[]{:T(128)}, f32[1024]{0:T(1024)S(1)}, f32[1024,256]{1,0:T(8,128)S(1)}, f32[]{:T(128)}, f32[2,256,256]{2,1,0:T(8,128)}, /*index=5*/s32[2]{0:T(1...) while((s32[]{:T(128)}, f32[1024]{0:T(1024)S(1)}, ...), condition=%wide.region_26.27_spmd.clone, body=%wide.region_22.26_spmd.clone.sunk | while | flops 406520576 | bytes 5407486 | solution.py:43
  334.7 9.3 %while.165 = (s32[]{:T(128)}, f32[1024]{0:T(1024)S(1)}, f32[1024,256]{1,0:T(8,128)S(1)}, f32[2,256,256]{2,1,0:T(8,128)}, s32[2]{0:T(128)S(1)}, /*index=5*/f32[51...) while((s32[]{:T(128)}, f32[1024]{0:T(1024)S(1)}, ...), condition=%wide.region_50.51_spmd.clone, body=%wide.region_47.50_spmd.clone.sunk | while | flops 406258432 | bytes 7504642 | solution.py:43
  344.1 2.6 select_add_fusion.7
  346.7 3.6 collective-permute-start.11
  350.3 2.7 select_add_fusion.6
  353.0 50.3 %psum.7 = f32[1]{0:T(128)} all-reduce(f32[1]{0:T(128)} %bitcast.4), channel_id=1, replica_groups=mesh['sys'=2,'blk'=8] {'blk'}, use_global_device_ids=true, to_apply=%region_27.28 | all-reduce | flops 1 | bytes 8 | tf_op jit(solution)/shard_map/psum | solution.py:109
  403.3 4.5 %multiply_add_fusion = (f32[1024,256]{1,0:T(8,128)}, f32[1024,256]{1,0:T(8,128)S(1)}, f32[1024,256]{1,0:T(8,128)S(1)}) fusion(f32[1024,256]{1,0:T(8,128)} %param.24, f32[1024,256]{1,0:T(8,128)} %collective-permute-done.16, f32[1024,256]{1,0:T(8,128)} %copy-done.2, f32[1024,256]{1,0:T(8,128)S(1)} %get-tuple-element.608, ...), kind=kLoop, calls=%fused_computation.172 | loop fusion | flops 4194304 | bytes 12591105 | tf_op jit(solution)/shard_map/add | solution.py:110
  (385 shorter events, 284.0 us)
Async XLA Ops:
  3.7 53.6 %collective-permute-start.7 = (bf16[1024,256]{1,0:T(8,128)(2,1)}, bf16[1024,256]{1,0:T(8,128)(2,1)}, u32[]{:S(2)}, u32[]{:S(2)}) collective-permute-start(bf16[1024,256]{1,0:T(8,128)(2,1)} %get-tuple-element.2135), channel_id=1, source_target_pairs={{0,1},{1,2},{2,3},{3,4},{4,5},{5,6},{6,7},{7,0},{8,9},{9,10},{10,1... | collective-permute-start | bytes 1572872 | tf_op jit(solution)/shard_map/ppermute | solution.py:64
  6.4 50.9 %collective-permute-start.6 = (f32[1024]{0:T(1024)}, f32[1024]{0:T(1024)S(1)}, u32[]{:S(2)}, u32[]{:S(2)}) collective-permute-start(f32[1024]{0:T(1024)} %param.25), channel_id=1, source_target_pairs={{0,1},{1,2},{2,3},{3,4},{4,5},{5,6},{6,7},{7,0},{8,9},{9,10},{10,1... | collective-permute-start | bytes 12296 | tf_op jit(solution)/shard_map/ppermute | solution.py:65
  6.4 183.7 %collective-permute-start.12 = (bf16[1024,256]{1,0:T(8,128)(2,1)}, bf16[1024,256]{1,0:T(8,128)(2,1)}, u32[]{:S(2)}, u32[]{:S(2)}) collective-permute-start(bf16[1024,256]{1,0:T(8,128)(2,1)} %get-tuple-element.2014), channel_id=1, source_target_pairs={{0,1},{1,2},{2,3},{3,4},{4,5},{5,6},{6,7},{7,0},{8,9},{9,10},{10,1... | collective-permute-start | bytes 1572872 | tf_op jit(solution)/shard_map/ppermute | solution.py:64
  94.4 6.2 %collective-permute-start.4 = (bf16[1024,256]{1,0:T(8,128)(2,1)}, bf16[1024,256]{1,0:T(8,128)(2,1)S(1)}, u32[]{:S(2)}, u32[]{:S(2)}) collective-permute-start(bf16[1024,256]{1,0:T(8,128)(2,1)} %get-tuple-element.2147), channel_id=1, source_target_pairs={{0,1},{1,2},{2,3},{3,4},{4,5},{5,6},{6,7},{7,0},{8,9},{9,10},{10,1... | collective-permute-start | bytes 1572872 | tf_op jit(solution)/shard_map/while/body/eval_jaxpr/ppermute | solution.py:72
  94.4 6.1 %collective-permute-start.3 = (f32[1024]{0:T(1024)S(1)}, f32[1024]{0:T(1024)S(1)}, u32[]{:S(2)}, u32[]{:S(2)}) collective-permute-start(f32[1024]{0:T(1024)S(1)} %get-tuple-element.2148), channel_id=1, source_target_pairs={{0,1},{1,2},{2,3},{3,4},{4,5},{5,6},{6,7},{7,0},{8,9},{9,10},{10,1... | collective-permute-start | bytes 12296 | tf_op jit(solution)/shard_map/while/body/eval_jaxpr/ppermute | solution.py:73
  95.8 41.5 %collective-permute-start.5 = (f32[1024,256]{1,0:T(8,128)}, f32[1024,256]{1,0:T(8,128)}, u32[]{:S(2)}, u32[]{:S(2)}) collective-permute-start(f32[1024,256]{1,0:T(8,128)} %get-tuple-element.2149), channel_id=1, source_target_pairs={{0,1},{1,2},{2,3},{3,4},{4,5},{5,6},{6,7},{7,0},{8,9},{9,10},{10,1... | collective-permute-start | bytes 3145736 | tf_op jit(solution)/shard_map/while/body/eval_jaxpr/ppermute | solution.py:74
  139.7 8.6 %collective-permute-start.4 = (bf16[1024,256]{1,0:T(8,128)(2,1)}, bf16[1024,256]{1,0:T(8,128)(2,1)S(1)}, u32[]{:S(2)}, u32[]{:S(2)}) collective-permute-start(bf16[1024,256]{1,0:T(8,128)(2,1)} %get-tuple-element.2147), channel_id=1, source_target_pairs={{0,1},{1,2},{2,3},{3,4},{4,5},{5,6},{6,7},{7,0},{8,9},{9,10},{10,1... | collective-permute-start | bytes 1572872 | tf_op jit(solution)/shard_map/while/body/eval_jaxpr/ppermute | solution.py:72
  142.2 6.1 %collective-permute-start.3 = (f32[1024]{0:T(1024)S(1)}, f32[1024]{0:T(1024)S(1)}, u32[]{:S(2)}, u32[]{:S(2)}) collective-permute-start(f32[1024]{0:T(1024)S(1)} %get-tuple-element.2148), channel_id=1, source_target_pairs={{0,1},{1,2},{2,3},{3,4},{4,5},{5,6},{6,7},{7,0},{8,9},{9,10},{10,1... | collective-permute-start | bytes 12296 | tf_op jit(solution)/shard_map/while/body/eval_jaxpr/ppermute | solution.py:73
  142.2 42.9 %collective-permute-start.5 = (f32[1024,256]{1,0:T(8,128)}, f32[1024,256]{1,0:T(8,128)}, u32[]{:S(2)}, u32[]{:S(2)}) collective-permute-start(f32[1024,256]{1,0:T(8,128)} %get-tuple-element.2149), channel_id=1, source_target_pairs={{0,1},{1,2},{2,3},{3,4},{4,5},{5,6},{6,7},{7,0},{8,9},{9,10},{10,1... | collective-permute-start | bytes 3145736 | tf_op jit(solution)/shard_map/while/body/eval_jaxpr/ppermute | solution.py:74
  187.5 129.3 %collective-permute-start.9 = (bf16[1024,256]{1,0:T(8,128)(2,1)}, bf16[1024,256]{1,0:T(8,128)(2,1)}, u32[]{:S(2)}, u32[]{:S(2)}) collective-permute-start(bf16[1024,256]{1,0:T(8,128)(2,1)} %get-tuple-element.592), channel_id=1, source_target_pairs={{0,1},{1,2},{2,3},{3,4},{4,5},{5,6},{6,7},{7,0},{8,9},{9,10},{10,1... | collective-permute-start | bytes 1572872 | tf_op jit(solution)/shard_map/ppermute | solution.py:80
  190.0 122.6 %collective-permute-start.8 = (f32[1024]{0:T(1024)S(1)}, f32[1024]{0:T(1024)S(1)}, u32[]{:S(2)}, u32[]{:S(2)}) collective-permute-start(f32[1024]{0:T(1024)S(1)} %get-tuple-element.591), channel_id=1, source_target_pairs={{0,1},{1,2},{2,3},{3,4},{4,5},{5,6},{6,7},{7,0},{8,9},{9,10},{10,1... | collective-permute-start | bytes 12296 | tf_op jit(solution)/shard_map/ppermute | solution.py:81
  226.8 7.5 %collective-permute-start.1 = (bf16[1024,256]{1,0:T(8,128)(2,1)}, bf16[1024,256]{1,0:T(8,128)(2,1)S(1)}, u32[]{:S(2)}, u32[]{:S(2)}) collective-permute-start(bf16[1024,256]{1,0:T(8,128)(2,1)} %get-tuple-element.2024), channel_id=1, source_target_pairs={{0,1},{1,2},{2,3},{3,4},{4,5},{5,6},{6,7},{7,0},{8,9},{9,10},{10,1... | collective-permute-start | bytes 1572872 | tf_op jit(solution)/shard_map/while/body/eval_jaxpr/ppermute | solution.py:72
  228.2 6.1 %collective-permute-start = (f32[1024]{0:T(1024)S(1)}, f32[1024]{0:T(1024)S(1)}, u32[]{:S(2)}, u32[]{:S(2)}) collective-permute-start(f32[1024]{0:T(1024)S(1)} %get-tuple-element.2025), channel_id=1, source_target_pairs={{0,1},{1,2},{2,3},{3,4},{4,5},{5,6},{6,7},{7,0},{8,9},{9,10},{10,1... | collective-permute-start | bytes 12296 | tf_op jit(solution)/shard_map/while/body/eval_jaxpr/ppermute | solution.py:73
  228.3 37.0 %collective-permute-start.2 = (f32[1024,256]{1,0:T(8,128)}, f32[1024,256]{1,0:T(8,128)}, u32[]{:S(2)}, u32[]{:S(2)}) collective-permute-start(f32[1024,256]{1,0:T(8,128)} %get-tuple-element.2026), channel_id=1, source_target_pairs={{0,1},{1,2},{2,3},{3,4},{4,5},{5,6},{6,7},{7,0},{8,9},{9,10},{10,1... | collective-permute-start | bytes 3145736 | tf_op jit(solution)/shard_map/while/body/eval_jaxpr/ppermute | solution.py:74
  267.7 8.7 %collective-permute-start.1 = (bf16[1024,256]{1,0:T(8,128)(2,1)}, bf16[1024,256]{1,0:T(8,128)(2,1)S(1)}, u32[]{:S(2)}, u32[]{:S(2)}) collective-permute-start(bf16[1024,256]{1,0:T(8,128)(2,1)} %get-tuple-element.2024), channel_id=1, source_target_pairs={{0,1},{1,2},{2,3},{3,4},{4,5},{5,6},{6,7},{7,0},{8,9},{9,10},{10,1... | collective-permute-start | bytes 1572872 | tf_op jit(solution)/shard_map/while/body/eval_jaxpr/ppermute | solution.py:72
  270.2 6.1 %collective-permute-start = (f32[1024]{0:T(1024)S(1)}, f32[1024]{0:T(1024)S(1)}, u32[]{:S(2)}, u32[]{:S(2)}) collective-permute-start(f32[1024]{0:T(1024)S(1)} %get-tuple-element.2025), channel_id=1, source_target_pairs={{0,1},{1,2},{2,3},{3,4},{4,5},{5,6},{6,7},{7,0},{8,9},{9,10},{10,1... | collective-permute-start | bytes 12296 | tf_op jit(solution)/shard_map/while/body/eval_jaxpr/ppermute | solution.py:73
  270.2 37.0 %collective-permute-start.2 = (f32[1024,256]{1,0:T(8,128)}, f32[1024,256]{1,0:T(8,128)}, u32[]{:S(2)}, u32[]{:S(2)}) collective-permute-start(f32[1024,256]{1,0:T(8,128)} %get-tuple-element.2026), channel_id=1, source_target_pairs={{0,1},{1,2},{2,3},{3,4},{4,5},{5,6},{6,7},{7,0},{8,9},{9,10},{10,1... | collective-permute-start | bytes 3145736 | tf_op jit(solution)/shard_map/while/body/eval_jaxpr/ppermute | solution.py:74
  309.6 5.8 %collective-permute-start.13 = (f32[1024]{0:T(1024)S(1)}, f32[1024]{0:T(1024)S(1)}, u32[]{:S(2)}, u32[]{:S(2)}) collective-permute-start(f32[1024]{0:T(1024)S(1)} %get-tuple-element.604), channel_id=1, source_target_pairs={{0,1},{1,2},{2,3},{3,4},{4,5},{5,6},{6,7},{7,0},{8,9},{9,10},{10,1... | collective-permute-start | bytes 12296 | tf_op jit(solution)/shard_map/ppermute | solution.py:81
  312.1 32.0 %collective-permute-start.10 = (f32[1024,256]{1,0:T(8,128)}, f32[1024,256]{1,0:T(8,128)}, u32[]{:S(2)}, u32[]{:S(2)}) collective-permute-start(f32[1024,256]{1,0:T(8,128)} %get-tuple-element.596), channel_id=1, source_target_pairs={{0,1},{1,2},{2,3},{3,4},{4,5},{5,6},{6,7},{7,0},{8,9},{9,10},{10,1... | collective-permute-start | bytes 3145736 | tf_op jit(solution)/shard_map/ppermute | solution.py:83
  312.2 18.4 %collective-permute-start.14 = (bf16[1024,256]{1,0:T(8,128)(2,1)}, bf16[1024,256]{1,0:T(8,128)(2,1)}, u32[]{:S(2)}, u32[]{:S(2)}) collective-permute-start(bf16[1024,256]{1,0:T(8,128)(2,1)} %get-tuple-element.605), channel_id=1, source_target_pairs={{0,1},{1,2},{2,3},{3,4},{4,5},{5,6},{6,7},{7,0},{8,9},{9,10},{10,1... | collective-permute-start | bytes 1572872 | tf_op jit(solution)/shard_map/ppermute | solution.py:80
  312.6 37.7 %collective-permute-start.15 = (f32[1024,256]{1,0:T(8,128)}, f32[1024,256]{1,0:T(8,128)}, u32[]{:S(2)}, u32[]{:S(2)}) collective-permute-start(f32[1024,256]{1,0:T(8,128)} %get-tuple-element.609), channel_id=1, source_target_pairs={{0,1},{1,2},{2,3},{3,4},{4,5},{5,6},{6,7},{7,0},{8,9},{9,10},{10,1... | collective-permute-start | bytes 3145736 | tf_op jit(solution)/shard_map/ppermute | solution.py:83
  346.7 56.6 %collective-permute-start.11 = (f32[1024,256]{1,0:T(8,128)}, f32[1024,256]{1,0:T(8,128)}, u32[]{:S(2)}, u32[]{:S(2)}) collective-permute-start(f32[1024,256]{1,0:T(8,128)} %select_add_fusion.7), channel_id=1, source_target_pairs={{0,4},{1,5},{2,6},{3,7},{4,0},{5,1},{6,2},{7,3},{8,12},{9,13},{10,... | collective-permute-start | bytes 3145736 | tf_op jit(solution)/shard_map/ppermute | solution.py:95
  350.3 53.0 %copy-start.1 = (f32[1024,256]{1,0:T(8,128)S(1)}, f32[1024,256]{1,0:T(8,128)}, u32[]{:S(2)}) copy-start(f32[1024,256]{1,0:T(8,128)} %copy-done) | copy-start | bytes 3145732
  353.0 50.3 %collective-permute-start.16 = (f32[1024,256]{1,0:T(8,128)}, f32[1024,256]{1,0:T(8,128)}, u32[]{:S(2)}, u32[]{:S(2)}) collective-permute-start(f32[1024,256]{1,0:T(8,128)} %select_add_fusion.6), channel_id=1, source_target_pairs={{0,4},{1,5},{2,6},{3,7},{4,0},{5,1},{6,2},{7,3},{8,12},{9,13},{10,... | collective-permute-start | bytes 3145736 | tf_op jit(solution)/shard_map/ppermute | solution.py:95
  (13 other events, 45.1 us)
where the time goes:
time: 415 us; the launch traced here: 409 us
  matrix products  166 us (40%)
  local copies, waits for them, and re-layouts  59.3 us (14%)
  other arithmetic  53.9 us (13%)
  blocking collectives  50.3 us (12%)
  loops' own time  37.2 us (9%)
  starting transfers between devices  25.2 us (6%)
  waiting for transfers between devices  17 us (4%)
    dot_general x36, matrix products, tile_step(): jnp.einsum('id,jd->ij', x_tile, x_b, preferred_element_type=jnp.float32)  71.3 us
    dot_general x36, matrix products, tile_step(): pull_sum = jnp.dot(w_low, x_b, preferred_element_type=jnp.float32)  59.3 us
    psum x1, blocking collectives, local_steps(): energy_one = lax.psum(energy_local, 'blk').reshape(1)  50.3 us
    another operation x10, loops' own time, block_pair(): lax.scan(tile_step, start_state, jnp.arange(rows_a // tile_rows))  36.9 us
    dot_general x28, matrix products, tile_step(): jnp.einsum('ij,id->jd', w_low, x_tile, preferred_element_type=jnp.float32)  34.9 us
    dynamic_slice x36, local copies, waits for them, and re-layouts, tile_step(): q_tile = lax.dynamic_slice_in_dim(q_a, row_start, tile_rows, 0)  24.6 us
    dynamic_slice x36, local copies, waits for them, and re-layouts, block_pair(): lax.scan(tile_step, start_state, jnp.arange(rows_a // tile_rows))  22.4 us
    ppermute x4, waiting for transfers between devices, pair_step(): q_seen = lax.ppermute(q_seen, 'blk', next_perm)  15.5 us
  transfers between devices with their start and end apart: 23, of which 5 were waited for; matrix products, arithmetic and copies ran while one was open for 65% of the time, Pallas kernels for 0%

commit v1 on v0

v1 whole, which is shorter than its diff:
```python
import functools
import math

import jax
import jax.numpy as jnp
from jax import lax
from jax.experimental import pallas as pl
from jax.experimental.pallas import tpu as pltpu
from jax.sharding import PartitionSpec as P

MESH = pl.DeviceIdType.MESH
STEP = 0.5
LOG2E = math.log2(math.e)
TILE = 256
LANES = 128
SIB, LEFT, RIGHT, LEFT_SIB, RIGHT_SIB, OPP, OPP_SIB = range(7)


def kernel(n, xs, vs, q_ref, f1_ref, e_ref, x2_ref, v2_ref,
           xg, mg, aw, qw, acc, rho, esend, ebuf,
           own_send, own_meta_send, fwd_send, fwd_meta_send, recv_sem, meta_recv, e_send, e_recv):
    rows, feat = xs.shape
    tiles = rows // TILE
    per = TILE // LANES
    half = tiles // 2
    me = lax.axis_index("blk")
    core = lax.rem(me, 2)
    sib = me + 1 - 2 * core
    right = lax.rem(me + 2, n)
    left = lax.rem(me + n - 2, n)
    opp = lax.rem(me + n // 2, n)
    left_sib = left + 1 - 2 * core
    right_sib = right + 1 - 2 * core
    opp_sib = opp + 1 - 2 * core

    def tile_rows(k):
        return pl.ds(k * TILE, TILE) if isinstance(k, int) else pl.ds(pl.multiple_of(k * TILE, TILE), TILE)

    def block_copy(e, k, blk, dev, send, rel):
        ref = xg.at[e, blk, tile_rows(k), :]
        return pltpu.make_async_remote_copy(src_ref=ref, dst_ref=ref, send_sem=send, recv_sem=recv_sem.at[rel, e, k],
                                            device_id={"blk": dev}, device_id_type=MESH)

    def meta_copy(blk, dev, send, rel):
        ref = mg.at[blk]
        return pltpu.make_async_remote_copy(src_ref=ref, dst_ref=ref, send_sem=send, recv_sem=meta_recv.at[rel],
                                            device_id={"blk": dev}, device_id_type=MESH)

    def own_copies(e, k):
        return (block_copy(e, k, me, right, own_send.at[0, e, k], LEFT),
                block_copy(e, k, me, left, own_send.at[1, e, k], RIGHT),
                block_copy(e, k, me, sib, own_send.at[2, e, k], SIB))

    def own_meta():
        return (meta_copy(me, right, own_meta_send.at[0], LEFT),
                meta_copy(me, left, own_meta_send.at[1], RIGHT),
                meta_copy(me, sib, own_meta_send.at[2], SIB))

    def fwd_left(e, k):
        return block_copy(e, k, left, sib, fwd_send.at[0, e, k], LEFT_SIB)

    def fwd_right(e, k):
        return block_copy(e, k, right, sib, fwd_send.at[1, e, k], RIGHT_SIB)

    def fwd_opp(e, k):
        return block_copy(e, k, opp, sib, fwd_send.at[2, e, k], OPP_SIB)

    def pass_right(e, k):
        return block_copy(e, k, left, right, fwd_send.at[3, e, k], OPP)

    def pass_left(e, k):
        return block_copy(e, k, right, left, fwd_send.at[3, e, k], OPP)

    def fwd_meta():
        return (meta_copy(left, sib, fwd_meta_send.at[0], LEFT_SIB),
                meta_copy(right, sib, fwd_meta_send.at[1], RIGHT_SIB),
                meta_copy(left, right, fwd_meta_send.at[2], OPP))

    def fwd_opp_meta():
        return meta_copy(opp, sib, fwd_meta_send.at[3], OPP_SIB)

    def arrived(e, k, blk, rel):
        block_copy(e, k, blk, sib, own_send.at[0, e, k], rel).wait_recv()

    def meta_arrived(blk, rel):
        meta_copy(blk, sib, own_meta_send.at[0], rel).wait_recv()

    def energy_copy(i):
        return pltpu.make_async_remote_copy(src_ref=esend, dst_ref=ebuf.at[me], send_sem=e_send.at[i], recv_sem=e_recv.at[i],
                                            device_id={"blk": lax.rem(me + i, n)}, device_id_type=MESH)

    def pair_tiles(e, pieces, masked):
        scale = LOG2E / feat
        cols = []
        for blk, k in pieces:
            b_j = xg[e, blk, tile_rows(k), :]
            a_j = jnp.concatenate([mg[blk, e, pl.ds(k * per + p, 1), :] for p in range(per)], axis=1)
            q_j = jnp.concatenate([mg[blk, 2, pl.ds(k * per + p, 1), :] for p in range(per)], axis=1)
            cols.append((b_j, a_j, q_j))
        for t in range(tiles):
            sl = tile_rows(t)
            x_t = xg[e, me, sl, :]
            a_t = jnp.concatenate([aw[e, sl, :]] * per, axis=1)
            q_t = jnp.concatenate([qw[sl, :]] * per, axis=1)
            rho_t = rho[e, sl, :]
            pull = None
            for p, (b_j, a_j, q_j) in enumerate(cols):
                g = lax.dot_general(x_t, b_j, (((1,), (1,)), ((), ())), preferred_element_type=jnp.float32)
                w = jnp.exp2(jnp.minimum(g * scale - a_t - a_j, 0.0)) * (q_t * q_j)
                if masked and p == t:
                    diag = lax.broadcasted_iota(jnp.int32, (TILE, TILE), 0) == lax.broadcasted_iota(jnp.int32, (TILE, TILE), 1)
                    w = jnp.where(diag, 0.0, w)
                for h in range(per):
                    rho_t = rho_t + w[:, h * LANES:(h + 1) * LANES]
                part = jnp.dot(w.astype(jnp.bfloat16), b_j, preferred_element_type=jnp.float32)
                pull = part if pull is None else pull + part
            rho[e, sl, :] = rho_t
            acc[e, sl, :] += pull

    def force(e, sl):
        rho_sum = jnp.sum(rho[e, sl, :], axis=1, keepdims=True)
        return (rho_sum * xg[e, me, sl, :].astype(jnp.float32) - acc[e, sl, :]) / feat

    barrier = pltpu.get_barrier_semaphore()
    for i in range(1, n):
        pl.semaphore_signal(barrier, inc=1, device_id={"blk": lax.rem(me + i, n)}, device_id_type=MESH)
    acc[...] = jnp.zeros_like(acc)
    rho[...] = jnp.zeros_like(rho)
    mg[me, 2] = q_ref[...]
    for k in range(tiles * per):
        qw[k * LANES:(k + 1) * LANES, :] = jnp.broadcast_to(q_ref[k:k + 1, :], (LANES, LANES)).T
    for k in range(tiles):
        sl = tile_rows(k)
        x1 = xs[sl, :] + STEP * vs[sl, :]
        xg[1, me, sl, :] = x1.astype(jnp.bfloat16)
        xg[0, me, sl, :] = xs[sl, :].astype(jnp.bfloat16)
        for e in (1, 0):
            b = xg[e, me, sl, :].astype(jnp.float32)
            s = jnp.sum(b * b, axis=1, keepdims=True) * (LOG2E / (2.0 * feat))
            aw[e, sl, :] = jnp.broadcast_to(s, (TILE, LANES))
            for p in range(per):
                r = k * per + p
                mg[me, e, r:r + 1, :] = aw[e, r * LANES:(r + 1) * LANES, :].T[0:1, :]
        if k == 0:
            pl.semaphore_wait(barrier, n - 1)
        for copy in own_copies(1, k):
            copy.start()
    for copy in own_meta():
        copy.start()
    for k in range(tiles):
        for copy in own_copies(0, k):
            copy.start()

    @pl.loop(0, 2)
    def _(i):
        pair_tiles(1 - i, [(me, k) for k in range(tiles)], True)

    meta_arrived(sib, SIB)

    @pl.loop(0, 2)
    def _(i):
        e = 1 - i
        for k in range(tiles):
            arrived(e, k, sib, SIB)
        pair_tiles(e, [(sib, k) for k in range(tiles)], False)

    meta_arrived(left, LEFT)
    meta_arrived(right, RIGHT)
    for copy in fwd_meta():
        copy.start()
    meta_arrived(left_sib, LEFT_SIB)
    meta_arrived(right_sib, RIGHT_SIB)

    @pl.loop(0, 2 * tiles)
    def _(i):
        e = 1 - i // tiles
        k = lax.rem(i, tiles)
        arrived(e, k, left, LEFT)
        fwd_left(e, k).start()

        @pl.when(k < half)
        def _():
            pass_right(e, k).start()

        arrived(e, k, right, RIGHT)
        fwd_right(e, k).start()

        @pl.when(k >= half)
        def _():
            pass_left(e, k).start()

        arrived(e, k, left_sib, LEFT_SIB)
        arrived(e, k, right_sib, RIGHT_SIB)
        pair_tiles(e, [(left, k), (right, k), (left_sib, k), (right_sib, k)], False)

    meta_arrived(opp, OPP)
    fwd_opp_meta().start()
    meta_arrived(opp_sib, OPP_SIB)

    def opposite(e, k):
        for t in (k, k + half):
            arrived(e, t, opp, OPP)
            fwd_opp(e, t).start()
        for t in (k, k + half):
            arrived(e, t, opp_sib, OPP_SIB)
        pair_tiles(e, [(opp, k), (opp, k + half), (opp_sib, k), (opp_sib, k + half)], False)

    @pl.loop(0, half)
    def _(k):
        opposite(1, k)

    part = jnp.zeros((8, LANES), jnp.float32)
    for r in range(rows // 8):
        part = part + rho[1, r * 8:(r + 1) * 8, :]
    esend[...] = part
    ebuf[me] = part
    for t in range(tiles):
        sl = tile_rows(t)
        f1_ref[sl, :] = force(1, sl)
    for i in range(1, n):
        energy_copy(i).start()

    @pl.loop(0, half)
    def _(k):
        opposite(0, k)

    for i in range(1, n):
        energy_copy(i).wait_recv()
    total = ebuf[0]
    for b in range(1, n):
        total = total + ebuf[b]
    e_ref[0] = 0.5 * jnp.sum(total)

    for t in range(tiles):
        sl = tile_rows(t)
        v1 = vs[sl, :] + STEP * force(0, sl)
        x2_ref[sl, :] = (xs[sl, :] + STEP * vs[sl, :]) + STEP * v1
        v2_ref[sl, :] = v1 + STEP * f1_ref[sl, :]

    for i in range(1, n):
        energy_copy(i).wait_send()
    for copy in own_meta() + fwd_meta() + (fwd_opp_meta(),):
        copy.wait_send()

    @pl.loop(0, 2 * tiles)
    def _(i):
        e = 1 - i // tiles
        k = lax.rem(i, tiles)
        for copy in own_copies(e, k) + (fwd_left(e, k), fwd_right(e, k), fwd_opp(e, k), pass_right(e, k)):
            copy.wait_send()


def solution(mesh):
    n = mesh.shape["blk"]
    row_spec = P(("sys", "blk"), None)
    vec_spec = P(("sys", "blk"))

    def local_steps(positions, velocity, charges):
        rows, feat = positions.shape
        tiles = rows // TILE
        block = jax.ShapeDtypeStruct((rows, feat), jnp.float32)
        vmem = pl.BlockSpec(memory_space=pltpu.VMEM)
        dma = pltpu.SemaphoreType.DMA
        force_one, energy_one, pos_two, vel_two = pl.pallas_call(
            functools.partial(kernel, n),
            out_shape=(block, jax.ShapeDtypeStruct((1,), jnp.float32), block, block),
            in_specs=[vmem, vmem, vmem],
            out_specs=(vmem, pl.BlockSpec(memory_space=pltpu.SMEM), vmem, vmem),
            scratch_shapes=[
                pltpu.VMEM((2, n, rows, feat), jnp.bfloat16),
                pltpu.VMEM((n, 3, rows // LANES, LANES), jnp.float32),
                pltpu.VMEM((2, rows, LANES), jnp.float32),
                pltpu.VMEM((rows, LANES), jnp.float32),
                pltpu.VMEM((2, rows, feat), jnp.float32),
                pltpu.VMEM((2, rows, LANES), jnp.float32),
                pltpu.VMEM((8, LANES), jnp.float32),
                pltpu.VMEM((n, 8, LANES), jnp.float32),
                dma((3, 2, tiles)),
                dma((3,)),
                dma((4, 2, tiles)),
                dma((4,)),
                dma((7, 2, tiles)),
                dma((7,)),
                dma((n,)),
                dma((n,)),
            ],
            compiler_params=pltpu.CompilerParams(collective_id=0, has_side_effects=True, vmem_limit_bytes=40 * 2**20),
            cost_estimate=pl.CostEstimate(flops=8 * n * rows * rows * feat, bytes_accessed=20 * rows * feat, transcendentals=2 * n * rows * rows),
        )(positions, velocity, charges.reshape(rows // LANES, LANES))
        return force_one, energy_one, pos_two, vel_two

    return jax.shard_map(local_steps, mesh=mesh, in_specs=(row_spec, row_spec, vec_spec), out_specs=(row_spec, P("sys"), row_spec, row_spec), check_vma=False)
```

time: 415 us -> 66.7 us (0.16); the launches traced: 409 us -> 66.1 us
  matrix products: 166 us -> 0 us
  Pallas kernels: 0 us -> 57.6 us
  other arithmetic: 53.9 us -> 0 us
  local copies, waits for them, and re-layouts: 59.3 us -> 6.04 us
  blocking collectives: 50.3 us -> 0 us
  loops' own time: 37.2 us -> 0 us
  starting transfers between devices: 25.2 us -> 0 us
  waiting for transfers between devices: 17 us -> 0 us
    dot_general x100 -> x0, matrix products: 166 us -> none  [the longest x36 71.3 us: tile_step(): jnp.einsum('id,jd->ij', x_tile, x_b, preferred_element_type=jnp.float32)]
    pallas_call x0 -> x1, Pallas kernels: none -> 57.6 us  [local_steps(): pl.pallas_call(functools.partial(kernel, n), out_shape=(block, jax.ShapeD...]
    psum x1 -> x0, blocking collectives: 50.3 us -> none  [local_steps(): energy_one = lax.psum(energy_local, 'blk').reshape(1)]
    dynamic_slice x108 -> x0, local copies, waits for them, and re-layouts: 49.8 us -> none  [the longest x36 24.6 us: tile_step(): q_tile = lax.dynamic_slice_in_dim(q_a, row_start, tile_rows, 0)]
    another operation x12 -> x0, loops' own time: 37.2 us -> none  [the longest x10 36.9 us: block_pair(): lax.scan(tile_step, start_state, jnp.arange(rows_a // tile_rows))]
    add x50 -> x0, other arithmetic: 30.2 us -> none  [the longest x4 9.63 us: pair_step(): react_run + react_step]
    ppermute x23 -> x0, starting transfers between devices: 25.2 us -> none  [the longest x4 6.41 us: pair_step(): x_seen = lax.ppermute(x_seen, 'blk', next_perm)]
    reduce_sum x15 -> x0, other arithmetic: 17.9 us -> none  [the longest x7 10.5 us: block_pair(): sq_a = jnp.sum(jnp.square(x_a.astype(jnp.float32)), axis=1)]
  transfers between devices with their start and end apart: 23 -> 0, of which waited for: 5 -> 0; matrix products, arithmetic and copies ran while one was open for 65% -> 0% of each run, Pallas kernels for 0% -> 0%
where the time goes in v1:
time: 66.7 us; the launch traced here: 66.1 us
  Pallas kernels  57.6 us (86%)
  local copies, waits for them, and re-layouts  6.04 us (9%)
  between operations  2.39 us (4%)
    pallas_call x1, Pallas kernels, local_steps(): pl.pallas_call(functools.partial(kernel, n), out_shape=(block, jax.ShapeD...  57.6 us
    unnamed x9, local copies, waits for them, and re-layouts  6.04 us

profile of v1, /device:TPU:113, one launch (start us, length us, event | category | flops | bytes accessed | tf_op | source)
XLA Modules:
  0.0 66.1 jit_solution(12197633514699058004)
XLA Ops:
  0.6 0.0 copy-start
  0.6 1.2 %copy-done = f32[1024,256]{1,0:T(8,128)S(1)} copy-done((f32[1024,256]{1,0:T(8,128)S(1)}, f32[1024,256]{1,0:T(8,128)}, u32[]{:S(2)}) %copy-start) | copy-done | bytes 1048600
  1.9 0.0 copy-start.1
  1.9 1.2 %copy-done.1 = f32[1024,256]{1,0:T(8,128)S(1)} copy-done((f32[1024,256]{1,0:T(8,128)S(1)}, f32[1024,256]{1,0:T(8,128)}, u32[]{:S(2)}) %copy-start.1) | copy-done | bytes 1048600
  3.1 0.0 copy-start.2
  3.1 0.7 %copy-done.2 = f32[1024]{0:T(1024)S(1)} copy-done((f32[1024]{0:T(1024)S(1)}, f32[1024]{0:T(1024)}, u32[]{:S(2)}) %copy-start.2) | copy-done | bytes 4120
  3.8 57.6 %shard_map.66 = (f32[1024,256]{1,0:T(8,128)S(1)}, f32[1]{0:T(128)}, f32[1024,256]{1,0:T(8,128)S(1)}, f32[1024,256]{1,0:T(8,128)S(1)}) custom-call(f32[1024,256]{1,0:T(8,128)S(1)} %copy-done, f32[1024,256]{1,0:T(8,128)S(1)} %copy-done.1, f32[8,128]{1,0:T(8,128)S(1)} %bitcast.1), custom_call_target="tpu_custom_call" | custom-call | flops 17179869184 | bytes 5242880 | tf_op jit(solution)/shard_map/pallas_call | solution.py:264
  61.4 1.0 %copy.11 = f32[1024,256]{1,0:T(8,128)} copy(f32[1024,256]{1,0:T(8,128)S(1)} %get-tuple-element.8) | data formatting | bytes 2097152
  63.0 1.0 %copy.13 = f32[1024,256]{1,0:T(8,128)} copy(f32[1024,256]{1,0:T(8,128)S(1)} %get-tuple-element.10) | data formatting | bytes 2097152
  64.0 1.0 %copy.14 = f32[1024,256]{1,0:T(8,128)} copy(f32[1024,256]{1,0:T(8,128)S(1)} %get-tuple-element.11) | data formatting | bytes 2097152
Async XLA Ops:
  0.6 1.2 %copy-start = (f32[1024,256]{1,0:T(8,128)S(1)}, f32[1024,256]{1,0:T(8,128)}, u32[]{:S(2)}) copy-start(f32[1024,256]{1,0:T(8,128)} %xs.1) | copy-start | bytes 3145732
  1.9 1.2 %copy-start.1 = (f32[1024,256]{1,0:T(8,128)S(1)}, f32[1024,256]{1,0:T(8,128)}, u32[]{:S(2)}) copy-start(f32[1024,256]{1,0:T(8,128)} %vs.1) | copy-start | bytes 3145732
  3.1 0.7 %copy-start.2 = (f32[1024]{0:T(1024)S(1)}, f32[1024]{0:T(1024)}, u32[]{:S(2)}) copy-start(f32[1024]{0:T(1024)} %param.5) | copy-start | bytes 12292

commit v2 on v1

--- a/solution.py
+++ b/solution.py
@@ -16,9 +16,9 @@
 SIB, LEFT, RIGHT, LEFT_SIB, RIGHT_SIB, OPP, OPP_SIB = range(7)
 
 
-def kernel(n, xs, vs, q_ref, f1_ref, e_ref, x2_ref, v2_ref,
-           xg, mg, aw, qw, acc, rho, esend, ebuf,
-           own_send, own_meta_send, fwd_send, fwd_meta_send, recv_sem, meta_recv, e_send, e_recv):
+def kernel(n, x0_hbm, v0_hbm, q_hbm, f1_ref, x2_ref, v2_ref, e_ref,
+           xs, vs, q_ref, xg, mg, aw, qw, acc, rho, esend, ebuf,
+           load_sem, q_sem, own_send, own_meta_send, fwd_send, fwd_meta_send, recv_sem, meta_recv, e_send, e_recv):
     rows, feat = xs.shape
     tiles = rows // TILE
     per = TILE // LANES
@@ -89,7 +89,11 @@
         return pltpu.make_async_remote_copy(src_ref=esend, dst_ref=ebuf.at[me], send_sem=e_send.at[i], recv_sem=e_recv.at[i],
                                             device_id={"blk": lax.rem(me + i, n)}, device_id_type=MESH)
 
-    def pair_tiles(e, pieces, masked):
+    def load(k, which):
+        src, dst = ((x0_hbm, xs), (v0_hbm, vs))[which]
+        return pltpu.make_async_copy(src.at[tile_rows(k), :], dst.at[tile_rows(k), :], load_sem.at[which, k])
+
+    def pair_tiles(e, pieces, masked=False, finish=None):
         scale = LOG2E / feat
         cols = []
         for blk, k in pieces:
@@ -114,46 +118,59 @@
                     rho_t = rho_t + w[:, h * LANES:(h + 1) * LANES]
                 part = jnp.dot(w.astype(jnp.bfloat16), b_j, preferred_element_type=jnp.float32)
                 pull = part if pull is None else pull + part
-            rho[e, sl, :] = rho_t
-            acc[e, sl, :] += pull
-
-    def force(e, sl):
-        rho_sum = jnp.sum(rho[e, sl, :], axis=1, keepdims=True)
-        return (rho_sum * xg[e, me, sl, :].astype(jnp.float32) - acc[e, sl, :]) / feat
+            pull = acc[e, sl, :] + pull
+            if finish is None:
+                rho[e, sl, :] = rho_t
+                acc[e, sl, :] = pull
+            else:
+                finish(sl, force(e, sl, rho_t, pull))
+
+    def force(e, sl, rho_t, pull):
+        rho_sum = jnp.sum(rho_t, axis=1, keepdims=True)
+        return (rho_sum * xg[e, me, sl, :].astype(jnp.float32) - pull) / feat
 
     barrier = pltpu.get_barrier_semaphore()
     for i in range(1, n):
         pl.semaphore_signal(barrier, inc=1, device_id={"blk": lax.rem(me + i, n)}, device_id_type=MESH)
+    for k in range(tiles):
+        load(k, 0).start()
+        load(k, 1).start()
+    q_load = pltpu.make_async_copy(q_hbm, q_ref, q_sem)
+    q_load.start()
     acc[...] = jnp.zeros_like(acc)
     rho[...] = jnp.zeros_like(rho)
-    mg[me, 2] = q_ref[...]
-    for k in range(tiles * per):
-        qw[k * LANES:(k + 1) * LANES, :] = jnp.broadcast_to(q_ref[k:k + 1, :], (LANES, LANES)).T
     for k in range(tiles):
         sl = tile_rows(k)
+        load(k, 0).wait()
+        load(k, 1).wait()
         x1 = xs[sl, :] + STEP * vs[sl, :]
         xg[1, me, sl, :] = x1.astype(jnp.bfloat16)
         xg[0, me, sl, :] = xs[sl, :].astype(jnp.bfloat16)
-        for e in (1, 0):
-            b = xg[e, me, sl, :].astype(jnp.float32)
-            s = jnp.sum(b * b, axis=1, keepdims=True) * (LOG2E / (2.0 * feat))
-            aw[e, sl, :] = jnp.broadcast_to(s, (TILE, LANES))
-            for p in range(per):
-                r = k * per + p
-                mg[me, e, r:r + 1, :] = aw[e, r * LANES:(r + 1) * LANES, :].T[0:1, :]
         if k == 0:
             pl.semaphore_wait(barrier, n - 1)
         for copy in own_copies(1, k):
             copy.start()
-    for copy in own_meta():
-        copy.start()
+    q_load.wait()
+    mg[me, 2] = q_ref[...]
+    for k in range(tiles * per):
+        sl = slice(k * LANES, (k + 1) * LANES)
+        qw[sl, :] = jnp.broadcast_to(q_ref[k:k + 1, :], (LANES, LANES)).T
+        for e in (1, 0):
+            b = xg[e, me, sl, :].astype(jnp.float32)
+            s = jnp.sum(b * b, axis=1, keepdims=True) * (LOG2E / (2.0 * feat))
+            wide = jnp.broadcast_to(s, (LANES, LANES))
+            aw[e, sl, :] = wide
+            mg[me, e, k:k + 1, :] = wide.T[0:1, :]
     for k in range(tiles):
         for copy in own_copies(0, k):
             copy.start()
+        if k == 0:
+            for copy in own_meta():
+                copy.start()
 
     @pl.loop(0, 2)
     def _(i):
-        pair_tiles(1 - i, [(me, k) for k in range(tiles)], True)
+        pair_tiles(1 - i, [(me, k) for k in range(tiles)], masked=True)
 
     meta_arrived(sib, SIB)
 
@@ -162,80 +179,100 @@
         e = 1 - i
         for k in range(tiles):
             arrived(e, k, sib, SIB)
-        pair_tiles(e, [(sib, k) for k in range(tiles)], False)
+        pair_tiles(e, [(sib, k) for k in range(tiles)])
+
+    def receive_sides(i):
+        e, k = 1 - i // tiles, lax.rem(i, tiles)
+        arrived(e, k, left, LEFT)
+        fwd_left(e, k).start()
+
+        @pl.when(k < half)
+        def _():
+            pass_right(e, k).start()
+
+        arrived(e, k, right, RIGHT)
+        fwd_right(e, k).start()
+
+        @pl.when(k >= half)
+        def _():
+            pass_left(e, k).start()
+
+    def compute_sides(i):
+        e, k = 1 - i // tiles, lax.rem(i, tiles)
+        arrived(e, k, left_sib, LEFT_SIB)
+        arrived(e, k, right_sib, RIGHT_SIB)
+        pair_tiles(e, [(left, k), (right, k), (left_sib, k), (right_sib, k)])
+
+    def receive_opposite(e, k):
+        for t in (k, k + half):
+            arrived(e, t, opp, OPP)
+            fwd_opp(e, t).start()
+
+    def opposite_relayed(e, k):
+        for t in (k, k + half):
+            arrived(e, t, opp_sib, OPP_SIB)
+
+    def compute_opposite(e, k):
+        opposite_relayed(e, k)
+        pair_tiles(e, [(opp, k), (opp, k + half), (opp_sib, k), (opp_sib, k + half)])
 
     meta_arrived(left, LEFT)
     meta_arrived(right, RIGHT)
     for copy in fwd_meta():
         copy.start()
+    receive_sides(0)
     meta_arrived(left_sib, LEFT_SIB)
     meta_arrived(right_sib, RIGHT_SIB)
 
-    @pl.loop(0, 2 * tiles)
-    def _(i):
-        e = 1 - i // tiles
-        k = lax.rem(i, tiles)
-        arrived(e, k, left, LEFT)
-        fwd_left(e, k).start()
-
-        @pl.when(k < half)
-        def _():
-            pass_right(e, k).start()
-
-        arrived(e, k, right, RIGHT)
-        fwd_right(e, k).start()
-
-        @pl.when(k >= half)
-        def _():
-            pass_left(e, k).start()
-
-        arrived(e, k, left_sib, LEFT_SIB)
-        arrived(e, k, right_sib, RIGHT_SIB)
-        pair_tiles(e, [(left, k), (right, k), (left_sib, k), (right_sib, k)], False)
-
-    meta_arrived(opp, OPP)
-    fwd_opp_meta().start()
-    meta_arrived(opp_sib, OPP_SIB)
-
-    def opposite(e, k):
-        for t in (k, k + half):
-            arrived(e, t, opp, OPP)
-            fwd_opp(e, t).start()
-        for t in (k, k + half):
-            arrived(e, t, opp_sib, OPP_SIB)
-        pair_tiles(e, [(opp, k), (opp, k + half), (opp_sib, k), (opp_sib, k + half)], False)
-
-    @pl.loop(0, half)
-    def _(k):
-        opposite(1, k)
-
-    part = jnp.zeros((8, LANES), jnp.float32)
-    for r in range(rows // 8):
-        part = part + rho[1, r * 8:(r + 1) * 8, :]
-    esend[...] = part
-    ebuf[me] = part
-    for t in range(tiles):
-        sl = tile_rows(t)
-        f1_ref[sl, :] = force(1, sl)
-    for i in range(1, n):
-        energy_copy(i).start()
-
-    @pl.loop(0, half)
-    def _(k):
-        opposite(0, k)
-
+    @pl.loop(1, 2 * tiles + 1)
+    def _(i):
+        @pl.when(i < 2 * tiles)
+        def _():
+            receive_sides(i)
+
+        @pl.when(i == 2 * tiles)
+        def _():
+            meta_arrived(opp, OPP)
+            fwd_opp_meta().start()
+            receive_opposite(1, 0)
+            meta_arrived(opp_sib, OPP_SIB)
+
+        compute_sides(i - 1)
+
+    @pl.loop(1, 2 * half)
+    def _(i):
+        receive_opposite(1 - i // half, lax.rem(i, half))
+        compute_opposite(1 - (i - 1) // half, lax.rem(i - 1, half))
+
+        @pl.when(i == half)
+        def _():
+            part = jnp.zeros((8, LANES), jnp.float32)
+            for r in range(rows // 8):
+                part = part + rho[1, r * 8:(r + 1) * 8, :]
+            esend[...] = part
+            ebuf[me] = part
+            for t in range(tiles):
+                sl = tile_rows(t)
+                f1_ref[sl, :] = force(1, sl, rho[1, sl, :], acc[1, sl, :])
+            for p in range(1, n):
+                energy_copy(p).start()
+
+    last = half - 1
+    pair_tiles(0, [(opp, last), (opp, last + half)])
     for i in range(1, n):
         energy_copy(i).wait_recv()
     total = ebuf[0]
     for b in range(1, n):
         total = total + ebuf[b]
-    e_ref[0] = 0.5 * jnp.sum(total)
-
-    for t in range(tiles):
-        sl = tile_rows(t)
-        v1 = vs[sl, :] + STEP * force(0, sl)
+    e_ref[...] = total
+    opposite_relayed(0, last)
+
+    def finish(sl, f0):
+        v1 = vs[sl, :] + STEP * f0
         x2_ref[sl, :] = (xs[sl, :] + STEP * vs[sl, :]) + STEP * v1
         v2_ref[sl, :] = v1 + STEP * f1_ref[sl, :]
+
+    pair_tiles(0, [(opp_sib, last), (opp_sib, last + half)], finish=finish)
 
     for i in range(1, n):
         energy_copy(i).wait_send()
@@ -248,6 +285,16 @@
         k = lax.rem(i, tiles)
         for copy in own_copies(e, k) + (fwd_left(e, k), fwd_right(e, k), fwd_opp(e, k), pass_right(e, k)):
             copy.wait_send()
+
+
+def write_out(f1_ref, x2_ref, v2_ref, parts_ref, f1_hbm, e_ref, x2_hbm, v2_hbm, sem):
+    copies = [pltpu.make_async_copy(src, dst, sem.at[i])
+              for i, (src, dst) in enumerate(((f1_ref, f1_hbm), (x2_ref, x2_hbm), (v2_ref, v2_hbm)))]
+    for copy in copies:
+        copy.start()
+    e_ref[0] = 0.5 * jnp.sum(parts_ref[...])
+    for copy in copies:
+        copy.wait()
 
 
 def solution(mesh):
@@ -260,13 +307,17 @@
         tiles = rows // TILE
         block = jax.ShapeDtypeStruct((rows, feat), jnp.float32)
         vmem = pl.BlockSpec(memory_space=pltpu.VMEM)
+        hbm = pl.BlockSpec(memory_space=pltpu.HBM)
         dma = pltpu.SemaphoreType.DMA
-        force_one, energy_one, pos_two, vel_two = pl.pallas_call(
+        parts = pl.pallas_call(
             functools.partial(kernel, n),
-            out_shape=(block, jax.ShapeDtypeStruct((1,), jnp.float32), block, block),
-            in_specs=[vmem, vmem, vmem],
-            out_specs=(vmem, pl.BlockSpec(memory_space=pltpu.SMEM), vmem, vmem),
+            out_shape=(block, block, block, jax.ShapeDtypeStruct((8, LANES), jnp.float32)),
+            in_specs=[hbm, hbm, hbm],
+            out_specs=(vmem, vmem, vmem, vmem),
             scratch_shapes=[
+                pltpu.VMEM((rows, feat), jnp.float32),
+                pltpu.VMEM((rows, feat), jnp.float32),
+                pltpu.VMEM((rows // LANES, LANES), jnp.float32),
                 pltpu.VMEM((2, n, rows, feat), jnp.bfloat16),
                 pltpu.VMEM((n, 3, rows // LANES, LANES), jnp.float32),
                 pltpu.VMEM((2, rows, LANES), jnp.float32),
@@ -275,6 +326,8 @@
                 pltpu.VMEM((2, rows, LANES), jnp.float32),
                 pltpu.VMEM((8, LANES), jnp.float32),
                 pltpu.VMEM((n, 8, LANES), jnp.float32),
+                dma((2, tiles)),
+                dma,
                 dma((3, 2, tiles)),
                 dma((3,)),
                 dma((4, 2, tiles)),
@@ -284,9 +337,17 @@
                 dma((n,)),
                 dma((n,)),
             ],
-            compiler_params=pltpu.CompilerParams(collective_id=0, has_side_effects=True, vmem_limit_bytes=40 * 2**20),
+            compiler_params=pltpu.CompilerParams(collective_id=0, has_side_effects=True, vmem_limit_bytes=52800000),
             cost_estimate=pl.CostEstimate(flops=8 * n * rows * rows * feat, bytes_accessed=20 * rows * feat, transcendentals=2 * n * rows * rows),
         )(positions, velocity, charges.reshape(rows // LANES, LANES))
+        force_one, energy_one, pos_two, vel_two = pl.pallas_call(
+            write_out,
+            out_shape=(block, jax.ShapeDtypeStruct((1,), jnp.float32), block, block),
+            in_specs=[vmem] * 4,
+            out_specs=(hbm, pl.BlockSpec(memory_space=pltpu.SMEM), hbm, hbm),
+            scratch_shapes=[dma((3,))],
+            compiler_params=pltpu.CompilerParams(vmem_limit_bytes=2**20),
+        )(*parts)
         return force_one, energy_one, pos_two, vel_two
 
     return jax.shard_map(local_steps, mesh=mesh, in_specs=(row_spec, row_spec, vec_spec), out_specs=(row_spec, P("sys"), row_spec, row_spec), check_vma=False)

time: 66.7 us -> 53 us (0.79)
  Pallas kernels: 57.6 us -> 51.6 us
  local copies, waits for them, and re-layouts: 6.04 us -> 0.68 us
  between operations: 2.39 us -> 0.65 us
    pallas_call x1 -> x2, Pallas kernels: 57.6 us -> 51.6 us  [the longest x1 49.4 us: local_steps(): pl.pallas_call(functools.partial(kernel, n), out_shape=(block, block, blo...]
    unnamed x9 -> x2, local copies, waits for them, and re-layouts: 6.04 us -> 0.68 us
where the time goes in v2:
time: 53 us; the launch traced here: 52.9 us
  Pallas kernels  51.6 us (97%)
  local copies, waits for them, and re-layouts  0.68 us (1%)
  between operations  0.65 us (1%)
    pallas_call x1, Pallas kernels, local_steps(): pl.pallas_call(functools.partial(kernel, n), out_shape=(block, block, blo...  49.4 us
    pallas_call x1, Pallas kernels, local_steps(): pl.pallas_call(write_out, out_shape=(block, jax.ShapeDtypeStruct((1,), jn...  2.21 us

profile of v2, /device:TPU:113, one launch (start us, length us, event | category | flops | bytes accessed | tf_op | source)
XLA Modules:
  0.0 52.9 jit_solution(12811169094419225401)
XLA Ops:
  0.6 0.0 copy-start
  0.6 0.7 %copy-done = f32[1024]{0:T(1024)S(1)} copy-done((f32[1024]{0:T(1024)S(1)}, f32[1024]{0:T(1024)}, u32[]{:S(2)}) %copy-start) | copy-done | bytes 4120
  1.3 49.4 %shard_map.66 = (f32[1024,256]{1,0:T(8,128)S(1)}, f32[1024,256]{1,0:T(8,128)S(1)}, f32[1024,256]{1,0:T(8,128)S(1)}, f32[8,128]{1,0:T(8,128)S(1)}) custom-call(f32[1024,256]{1,0:T(8,128)} %x0_hbm.1, f32[1024,256]{1,0:T(8,128)} %v0_hbm.1, f32[8,128]{1,0:T(8,128)S(1)} %bitcast.1), custom_call_target="tpu_custom_call" | custom-call | flops 17179869184 | bytes 5242880 | tf_op jit(solution)/shard_map/pallas_call | solution.py:312
  50.7 2.2 %shard_map.67 = (f32[1024,256]{1,0:T(8,128)}, f32[1]{0:T(128)}, f32[1024,256]{1,0:T(8,128)}, f32[1024,256]{1,0:T(8,128)}) custom-call(f32[1024,256]{1,0:T(8,128)S(1)} %get-tuple-element.8.f1_ref, f32[1024,256]{1,0:T(8,128)S(1)} %get-tuple-element.9.x2_ref, f32[1024,256]{1,0:T(8,128)S(1)} %get-tuple-element.10.v2_ref, f32[8,128]{1,0:T(8,128)S(1)} %get-tuple-element.11.parts_ref), custom_call_target="tpu_custom_call" | custom-call | tf_op jit(solution)/shard_map/pallas_call | solution.py:343
Async XLA Ops:
  0.6 0.7 %copy-start = (f32[1024]{0:T(1024)S(1)}, f32[1024]{0:T(1024)}, u32[]{:S(2)}) copy-start(f32[1024]{0:T(1024)} %param.5) | copy-start | bytes 12292

commit v3 on v2

--- a/solution.py
+++ b/solution.py
@@ -148,25 +148,29 @@
         xg[0, me, sl, :] = xs[sl, :].astype(jnp.bfloat16)
         if k == 0:
             pl.semaphore_wait(barrier, n - 1)
-        for copy in own_copies(1, k):
-            copy.start()
+            for copy in own_copies(1, k):
+                copy.start()
     q_load.wait()
     mg[me, 2] = q_ref[...]
     for k in range(tiles * per):
         sl = slice(k * LANES, (k + 1) * LANES)
-        qw[sl, :] = jnp.broadcast_to(q_ref[k:k + 1, :], (LANES, LANES)).T
         for e in (1, 0):
             b = xg[e, me, sl, :].astype(jnp.float32)
             s = jnp.sum(b * b, axis=1, keepdims=True) * (LOG2E / (2.0 * feat))
             wide = jnp.broadcast_to(s, (LANES, LANES))
             aw[e, sl, :] = wide
             mg[me, e, k:k + 1, :] = wide.T[0:1, :]
+    for k in range(1, tiles):
+        for copy in own_copies(1, k):
+            copy.start()
+        if k == 1:
+            for copy in own_meta():
+                copy.start()
     for k in range(tiles):
         for copy in own_copies(0, k):
             copy.start()
-        if k == 0:
-            for copy in own_meta():
-                copy.start()
+    for k in range(tiles * per):
+        qw[k * LANES:(k + 1) * LANES, :] = jnp.broadcast_to(q_ref[k:k + 1, :], (LANES, LANES)).T
 
     @pl.loop(0, 2)
     def _(i):
@@ -197,52 +201,61 @@
         def _():
             pass_left(e, k).start()
 
-    def compute_sides(i):
+    def own_sides(i):
+        e, k = 1 - i // tiles, lax.rem(i, tiles)
+        pair_tiles(e, [(left, k), (right, k)])
+
+    def relayed_sides(i):
         e, k = 1 - i // tiles, lax.rem(i, tiles)
         arrived(e, k, left_sib, LEFT_SIB)
         arrived(e, k, right_sib, RIGHT_SIB)
-        pair_tiles(e, [(left, k), (right, k), (left_sib, k), (right_sib, k)])
+        pair_tiles(e, [(left_sib, k), (right_sib, k)])
 
     def receive_opposite(e, k):
         for t in (k, k + half):
             arrived(e, t, opp, OPP)
             fwd_opp(e, t).start()
 
-    def opposite_relayed(e, k):
+    def own_opposite(e, k):
+        pair_tiles(e, [(opp, k), (opp, k + half)])
+
+    def relayed_opposite(e, k, finish=None):
         for t in (k, k + half):
             arrived(e, t, opp_sib, OPP_SIB)
-
-    def compute_opposite(e, k):
-        opposite_relayed(e, k)
-        pair_tiles(e, [(opp, k), (opp, k + half), (opp_sib, k), (opp_sib, k + half)])
+        pair_tiles(e, [(opp_sib, k), (opp_sib, k + half)], finish=finish)
 
     meta_arrived(left, LEFT)
     meta_arrived(right, RIGHT)
     for copy in fwd_meta():
         copy.start()
-    receive_sides(0)
     meta_arrived(left_sib, LEFT_SIB)
     meta_arrived(right_sib, RIGHT_SIB)
 
-    @pl.loop(1, 2 * tiles + 1)
-    def _(i):
-        @pl.when(i < 2 * tiles)
-        def _():
-            receive_sides(i)
-
-        @pl.when(i == 2 * tiles)
-        def _():
-            meta_arrived(opp, OPP)
-            fwd_opp_meta().start()
-            receive_opposite(1, 0)
-            meta_arrived(opp_sib, OPP_SIB)
-
-        compute_sides(i - 1)
-
-    @pl.loop(1, 2 * half)
-    def _(i):
-        receive_opposite(1 - i // half, lax.rem(i, half))
-        compute_opposite(1 - (i - 1) // half, lax.rem(i - 1, half))
+    @pl.loop(0, 2 * tiles)
+    def _(i):
+        receive_sides(i)
+
+        @pl.when(i > 0)
+        def _():
+            relayed_sides(i - 1)
+
+        own_sides(i)
+
+    meta_arrived(opp, OPP)
+    fwd_opp_meta().start()
+    receive_opposite(1, 0)
+    relayed_sides(2 * tiles - 1)
+    meta_arrived(opp_sib, OPP_SIB)
+
+    @pl.loop(0, 2 * half - 1)
+    def _(i):
+        e, k = 1 - i // half, lax.rem(i, half)
+
+        @pl.when(i > 0)
+        def _():
+            receive_opposite(e, k)
+
+        own_opposite(e, k)
 
         @pl.when(i == half)
         def _():
@@ -251,28 +264,30 @@
                 part = part + rho[1, r * 8:(r + 1) * 8, :]
             esend[...] = part
             ebuf[me] = part
-            for t in range(tiles):
-                sl = tile_rows(t)
-                f1_ref[sl, :] = force(1, sl, rho[1, sl, :], acc[1, sl, :])
             for p in range(1, n):
                 energy_copy(p).start()
 
+        relayed_opposite(e, k)
+
     last = half - 1
-    pair_tiles(0, [(opp, last), (opp, last + half)])
+    receive_opposite(0, last)
+    own_opposite(0, last)
+    for t in range(tiles):
+        sl = tile_rows(t)
+        f1_ref[sl, :] = force(1, sl, rho[1, sl, :], acc[1, sl, :])
     for i in range(1, n):
         energy_copy(i).wait_recv()
     total = ebuf[0]
     for b in range(1, n):
         total = total + ebuf[b]
     e_ref[...] = total
-    opposite_relayed(0, last)
 
     def finish(sl, f0):
         v1 = vs[sl, :] + STEP * f0
         x2_ref[sl, :] = (xs[sl, :] + STEP * vs[sl, :]) + STEP * v1
         v2_ref[sl, :] = v1 + STEP * f1_ref[sl, :]
 
-    pair_tiles(0, [(opp_sib, last), (opp_sib, last + half)], finish=finish)
+    relayed_opposite(0, last, finish=finish)
 
     for i in range(1, n):
         energy_copy(i).wait_send()

time: 53 us -> 49.5 us (0.934)
  Pallas kernels: 51.6 us -> 48 us
    pallas_call x1, Pallas kernels: 49.4 us -> 45.8 us  [local_steps(): pl.pallas_call(functools.partial(kernel, n), out_shape=(block, block, blo...]
where the time goes in v3:
time: 49.5 us; the launch traced here: 49.3 us
  Pallas kernels  48 us (97%)
  local copies, waits for them, and re-layouts  0.68 us (1%)
  between operations  0.65 us (1%)
    pallas_call x1, Pallas kernels, local_steps(): pl.pallas_call(functools.partial(kernel, n), out_shape=(block, block, blo...  45.8 us
    pallas_call x1, Pallas kernels, local_steps(): pl.pallas_call(write_out, out_shape=(block, jax.ShapeDtypeStruct((1,), jn...  2.21 us

profile of v3, /device:TPU:113, one launch (start us, length us, event | category | flops | bytes accessed | tf_op | source)
XLA Modules:
  0.0 49.3 jit_solution(4090626771186331561)
XLA Ops:
  0.6 0.0 copy-start
  0.6 0.7 %copy-done = f32[1024]{0:T(1024)S(1)} copy-done((f32[1024]{0:T(1024)S(1)}, f32[1024]{0:T(1024)}, u32[]{:S(2)}) %copy-start) | copy-done | bytes 4120
  1.3 45.8 %shard_map.66 = (f32[1024,256]{1,0:T(8,128)S(1)}, f32[1024,256]{1,0:T(8,128)S(1)}, f32[1024,256]{1,0:T(8,128)S(1)}, f32[8,128]{1,0:T(8,128)S(1)}) custom-call(f32[1024,256]{1,0:T(8,128)} %x0_hbm.1, f32[1024,256]{1,0:T(8,128)} %v0_hbm.1, f32[8,128]{1,0:T(8,128)S(1)} %bitcast.1), custom_call_target="tpu_custom_call" | custom-call | flops 17179869184 | bytes 5242880 | tf_op jit(solution)/shard_map/pallas_call | solution.py:327
  47.1 2.2 %shard_map.67 = (f32[1024,256]{1,0:T(8,128)}, f32[1]{0:T(128)}, f32[1024,256]{1,0:T(8,128)}, f32[1024,256]{1,0:T(8,128)}) custom-call(f32[1024,256]{1,0:T(8,128)S(1)} %get-tuple-element.8.f1_ref, f32[1024,256]{1,0:T(8,128)S(1)} %get-tuple-element.9.x2_ref, f32[1024,256]{1,0:T(8,128)S(1)} %get-tuple-element.10.v2_ref, f32[8,128]{1,0:T(8,128)S(1)} %get-tuple-element.11.parts_ref), custom_call_target="tpu_custom_call" | custom-call | tf_op jit(solution)/shard_map/pallas_call | solution.py:358
Async XLA Ops:
  0.6 0.7 %copy-start = (f32[1024]{0:T(1024)S(1)}, f32[1024]{0:T(1024)}, u32[]{:S(2)}) copy-start(f32[1024]{0:T(1024)} %param.5) | copy-start | bytes 12292

commit v4 on v3

--- a/solution.py
+++ b/solution.py
@@ -247,6 +247,11 @@
     relayed_sides(2 * tiles - 1)
     meta_arrived(opp_sib, OPP_SIB)
 
+    def first_force(some):
+        for t in some:
+            sl = tile_rows(t)
+            f1_ref[sl, :] = force(1, sl, rho[1, sl, :], acc[1, sl, :])
+
     @pl.loop(0, 2 * half - 1)
     def _(i):
         e, k = 1 - i // half, lax.rem(i, half)
@@ -266,15 +271,14 @@
             ebuf[me] = part
             for p in range(1, n):
                 energy_copy(p).start()
+            first_force(range(half))
 
         relayed_opposite(e, k)
 
     last = half - 1
     receive_opposite(0, last)
     own_opposite(0, last)
-    for t in range(tiles):
-        sl = tile_rows(t)
-        f1_ref[sl, :] = force(1, sl, rho[1, sl, :], acc[1, sl, :])
+    first_force(range(half, tiles))
     for i in range(1, n):
         energy_copy(i).wait_recv()
     total = ebuf[0]
@@ -302,12 +306,13 @@
             copy.wait_send()
 
 
-def write_out(f1_ref, x2_ref, v2_ref, parts_ref, f1_hbm, e_ref, x2_hbm, v2_hbm, sem):
+def write_out(f1_ref, x2_ref, v2_ref, parts_ref, f1_hbm, e_hbm, x2_hbm, v2_hbm, e_ref, sem):
     copies = [pltpu.make_async_copy(src, dst, sem.at[i])
-              for i, (src, dst) in enumerate(((f1_ref, f1_hbm), (x2_ref, x2_hbm), (v2_ref, v2_hbm)))]
-    for copy in copies:
+              for i, (src, dst) in enumerate(((f1_ref, f1_hbm), (x2_ref, x2_hbm), (v2_ref, v2_hbm), (e_ref, e_hbm)))]
+    for copy in copies[:3]:
         copy.start()
     e_ref[0] = 0.5 * jnp.sum(parts_ref[...])
+    copies[3].start()
     for copy in copies:
         copy.wait()
 
@@ -354,13 +359,13 @@
             ],
             compiler_params=pltpu.CompilerParams(collective_id=0, has_side_effects=True, vmem_limit_bytes=52800000),
             cost_estimate=pl.CostEstimate(flops=8 * n * rows * rows * feat, bytes_accessed=20 * rows * feat, transcendentals=2 * n * rows * rows),
-        )(positions, velocity, charges.reshape(rows // LANES, LANES))
+        )(*[pltpu.with_memory_space_constraint(x, pltpu.HBM) for x in (positions, velocity, charges.reshape(rows // LANES, LANES))])
         force_one, energy_one, pos_two, vel_two = pl.pallas_call(
             write_out,
             out_shape=(block, jax.ShapeDtypeStruct((1,), jnp.float32), block, block),
             in_specs=[vmem] * 4,
-            out_specs=(hbm, pl.BlockSpec(memory_space=pltpu.SMEM), hbm, hbm),
-            scratch_shapes=[dma((3,))],
+            out_specs=(hbm, hbm, hbm, hbm),
+            scratch_shapes=[pltpu.SMEM((1,), jnp.float32), dma((4,))],
             compiler_params=pltpu.CompilerParams(vmem_limit_bytes=2**20),
         )(*parts)
         return force_one, energy_one, pos_two, vel_two

time: 49.5 us -> 48.5 us (0.980)
  local copies, waits for them, and re-layouts: 0.68 us -> 0 us
    unnamed x2 -> x0, local copies, waits for them, and re-layouts: 0.68 us -> none
    pallas_call x1, Pallas kernels: 2.21 us -> 1.71 us  [local_steps(): pl.pallas_call(write_out, out_shape=(block, jax.ShapeDtypeStruct((1,), jn...]
where the time goes in v4:
time: 48.5 us; the launch traced here: 48.4 us
  Pallas kernels  47.8 us (99%)
  between operations  0.64 us (1%)
    pallas_call x1, Pallas kernels, local_steps(): pl.pallas_call(functools.partial(kernel, n), out_shape=(block, block, blo...  46.1 us
    pallas_call x1, Pallas kernels, local_steps(): pl.pallas_call(write_out, out_shape=(block, jax.ShapeDtypeStruct((1,), jn...  1.71 us

profile of v4, /device:TPU:113, one launch (start us, length us, event | category | flops | bytes accessed | tf_op | source)
XLA Modules:
  0.0 48.4 jit_solution(10836320833213011952)
XLA Ops:
  0.6 46.1 %shard_map.66 = (f32[1024,256]{1,0:T(8,128)S(1)}, f32[1024,256]{1,0:T(8,128)S(1)}, f32[1024,256]{1,0:T(8,128)S(1)}, f32[8,128]{1,0:T(8,128)S(1)}) custom-call(f32[1024,256]{1,0:T(8,128)} %x0_hbm.1, f32[1024,256]{1,0:T(8,128)} %v0_hbm.1, f32[8,128]{1,0:T(8,128)} %bitcast.1), custom_call_target="tpu_custom_call" | custom-call | flops 17179869184 | bytes 5242880 | tf_op jit(solution)/shard_map/pallas_call | solution.py:332
  46.7 1.7 %shard_map.67 = (f32[1024,256]{1,0:T(8,128)}, f32[1]{0:T(128)}, f32[1024,256]{1,0:T(8,128)}, f32[1024,256]{1,0:T(8,128)}) custom-call(f32[1024,256]{1,0:T(8,128)S(1)} %get-tuple-element.8.f1_ref, f32[1024,256]{1,0:T(8,128)S(1)} %get-tuple-element.9.x2_ref, f32[1024,256]{1,0:T(8,128)S(1)} %get-tuple-element.10.v2_ref, f32[8,128]{1,0:T(8,128)S(1)} %get-tuple-element.11.parts_ref), custom_call_target="tpu_custom_call" | custom-call | tf_op jit(solution)/shard_map/pallas_call | solution.py:363

commit v5 on v4

--- a/solution.py
+++ b/solution.py
@@ -119,8 +119,8 @@
                 part = jnp.dot(w.astype(jnp.bfloat16), b_j, preferred_element_type=jnp.float32)
                 pull = part if pull is None else pull + part
             pull = acc[e, sl, :] + pull
+            rho[e, sl, :] = rho_t
             if finish is None:
-                rho[e, sl, :] = rho_t
                 acc[e, sl, :] = pull
             else:
                 finish(sl, force(e, sl, rho_t, pull))
@@ -132,13 +132,15 @@
     barrier = pltpu.get_barrier_semaphore()
     for i in range(1, n):
         pl.semaphore_signal(barrier, inc=1, device_id={"blk": lax.rem(me + i, n)}, device_id_type=MESH)
-    for k in range(tiles):
+    load(0, 0).start()
+    load(0, 1).start()
+    q_load = pltpu.make_async_copy(q_hbm, q_ref, q_sem)
+    rho[...] = jnp.zeros_like(rho)
+    for k in range(1, tiles):
         load(k, 0).start()
         load(k, 1).start()
-    q_load = pltpu.make_async_copy(q_hbm, q_ref, q_sem)
     q_load.start()
     acc[...] = jnp.zeros_like(acc)
-    rho[...] = jnp.zeros_like(rho)
     for k in range(tiles):
         sl = tile_rows(k)
         load(k, 0).wait()
@@ -201,28 +203,20 @@
         def _():
             pass_left(e, k).start()
 
-    def own_sides(i):
-        e, k = 1 - i // tiles, lax.rem(i, tiles)
-        pair_tiles(e, [(left, k), (right, k)])
-
-    def relayed_sides(i):
-        e, k = 1 - i // tiles, lax.rem(i, tiles)
+    def relayed_sides(e, k):
         arrived(e, k, left_sib, LEFT_SIB)
         arrived(e, k, right_sib, RIGHT_SIB)
-        pair_tiles(e, [(left_sib, k), (right_sib, k)])
+        return [(left_sib, k), (right_sib, k)]
 
     def receive_opposite(e, k):
         for t in (k, k + half):
             arrived(e, t, opp, OPP)
             fwd_opp(e, t).start()
 
-    def own_opposite(e, k):
-        pair_tiles(e, [(opp, k), (opp, k + half)])
-
-    def relayed_opposite(e, k, finish=None):
+    def relayed_opposite(e, k):
         for t in (k, k + half):
             arrived(e, t, opp_sib, OPP_SIB)
-        pair_tiles(e, [(opp_sib, k), (opp_sib, k + half)], finish=finish)
+        return [(opp_sib, k), (opp_sib, k + half)]
 
     meta_arrived(left, LEFT)
     meta_arrived(right, RIGHT)
@@ -233,37 +227,43 @@
 
     @pl.loop(0, 2 * tiles)
     def _(i):
+        e, k = 1 - i // tiles, lax.rem(i, tiles)
         receive_sides(i)
-
-        @pl.when(i > 0)
-        def _():
-            relayed_sides(i - 1)
-
-        own_sides(i)
+        sides = [(left, k), (right, k)]
+
+        @pl.when(k > 0)
+        def _():
+            pair_tiles(e, sides + relayed_sides(e, k - 1))
+
+        @pl.when(k == 0)
+        def _():
+            @pl.when(i > 0)
+            def _():
+                pair_tiles(1, relayed_sides(1, tiles - 1))
+
+            pair_tiles(e, sides)
+
+    def first_finish(sl, f1):
+        f1_ref[sl, :] = f1
+
+    def last_finish(sl, f0):
+        v1 = vs[sl, :] + STEP * f0
+        x2_ref[sl, :] = (xs[sl, :] + STEP * vs[sl, :]) + STEP * v1
+        v2_ref[sl, :] = v1 + STEP * f1_ref[sl, :]
 
     meta_arrived(opp, OPP)
     fwd_opp_meta().start()
     receive_opposite(1, 0)
-    relayed_sides(2 * tiles - 1)
+    pair_tiles(0, relayed_sides(0, tiles - 1))
     meta_arrived(opp_sib, OPP_SIB)
 
-    def first_force(some):
-        for t in some:
-            sl = tile_rows(t)
-            f1_ref[sl, :] = force(1, sl, rho[1, sl, :], acc[1, sl, :])
-
-    @pl.loop(0, 2 * half - 1)
-    def _(i):
-        e, k = 1 - i // half, lax.rem(i, half)
-
-        @pl.when(i > 0)
-        def _():
-            receive_opposite(e, k)
-
-        own_opposite(e, k)
-
-        @pl.when(i == half)
-        def _():
+    @pl.loop(0, 2)
+    def _(i):
+        e = 1 - i
+
+        @pl.when(i == 1)
+        def _():
+            pair_tiles(1, relayed_opposite(1, half - 1), finish=first_finish)
             part = jnp.zeros((8, LANES), jnp.float32)
             for r in range(rows // 8):
                 part = part + rho[1, r * 8:(r + 1) * 8, :]
@@ -271,27 +271,17 @@
             ebuf[me] = part
             for p in range(1, n):
                 energy_copy(p).start()
-            first_force(range(half))
-
-        relayed_opposite(e, k)
-
-    last = half - 1
-    receive_opposite(0, last)
-    own_opposite(0, last)
-    first_force(range(half, tiles))
+            receive_opposite(0, 0)
+
+        pair_tiles(e, [(opp, 0), (opp, half)])
+        for k in range(1, half):
+            receive_opposite(e, k)
+            pair_tiles(e, [(opp, k), (opp, k + half)] + relayed_opposite(e, k - 1))
+
+    pair_tiles(0, relayed_opposite(0, half - 1), finish=last_finish)
     for i in range(1, n):
         energy_copy(i).wait_recv()
-    total = ebuf[0]
-    for b in range(1, n):
-        total = total + ebuf[b]
-    e_ref[...] = total
-
-    def finish(sl, f0):
-        v1 = vs[sl, :] + STEP * f0
-        x2_ref[sl, :] = (xs[sl, :] + STEP * vs[sl, :]) + STEP * v1
-        v2_ref[sl, :] = v1 + STEP * f1_ref[sl, :]
-
-    relayed_opposite(0, last, finish=finish)
+    e_ref[...] = ebuf[...]
 
     for i in range(1, n):
         energy_copy(i).wait_send()
@@ -311,7 +301,10 @@
               for i, (src, dst) in enumerate(((f1_ref, f1_hbm), (x2_ref, x2_hbm), (v2_ref, v2_hbm), (e_ref, e_hbm)))]
     for copy in copies[:3]:
         copy.start()
-    e_ref[0] = 0.5 * jnp.sum(parts_ref[...])
+    total = parts_ref[0]
+    for b in range(1, parts_ref.shape[0]):
+        total = total + parts_ref[b]
+    e_ref[0] = 0.5 * jnp.sum(total)
     copies[3].start()
     for copy in copies:
         copy.wait()
@@ -331,7 +324,7 @@
         dma = pltpu.SemaphoreType.DMA
         parts = pl.pallas_call(
             functools.partial(kernel, n),
-            out_shape=(block, block, block, jax.ShapeDtypeStruct((8, LANES), jnp.float32)),
+            out_shape=(block, block, block, jax.ShapeDtypeStruct((n, 8, LANES), jnp.float32)),
             in_specs=[hbm, hbm, hbm],
             out_specs=(vmem, vmem, vmem, vmem),
             scratch_shapes=[

time: 48.5 us -> 47.5 us (0.979)
  Pallas kernels: 47.8 us -> 46.7 us
    pallas_call x1, Pallas kernels: 46.1 us -> 45 us  [local_steps(): pl.pallas_call(functools.partial(kernel, n), out_shape=(block, block, blo...]
where the time goes in v5:
time: 47.5 us; the launch traced here: 47.4 us
  Pallas kernels  46.7 us (98%)
  between operations  0.64 us (1%)
    pallas_call x1, Pallas kernels, local_steps(): pl.pallas_call(functools.partial(kernel, n), out_shape=(block, block, blo...  45 us
    pallas_call x1, Pallas kernels, local_steps(): pl.pallas_call(write_out, out_shape=(block, jax.ShapeDtypeStruct((1,), jn...  1.71 us

profile of v5, /device:TPU:113, one launch (start us, length us, event | category | flops | bytes accessed | tf_op | source)
XLA Modules:
  0.0 47.4 jit_solution(15474438436850922437)
XLA Ops:
  0.6 45.0 %shard_map.66 = (f32[1024,256]{1,0:T(8,128)S(1)}, f32[1024,256]{1,0:T(8,128)S(1)}, f32[1024,256]{1,0:T(8,128)S(1)}, f32[8,8,128]{2,1,0:T(8,128)S(1)}) custom-call(f32[1024,256]{1,0:T(8,128)} %x0_hbm.1, f32[1024,256]{1,0:T(8,128)} %v0_hbm.1, f32[8,128]{1,0:T(8,128)} %bitcast.1), custom_call_target="tpu_custom_call" | custom-call | flops 17179869184 | bytes 5242880 | tf_op jit(solution)/shard_map/pallas_call | solution.py:325
  45.7 1.7 %shard_map.67 = (f32[1024,256]{1,0:T(8,128)}, f32[1]{0:T(128)}, f32[1024,256]{1,0:T(8,128)}, f32[1024,256]{1,0:T(8,128)}) custom-call(f32[1024,256]{1,0:T(8,128)S(1)} %get-tuple-element.8.f1_ref, f32[1024,256]{1,0:T(8,128)S(1)} %get-tuple-element.9.x2_ref, f32[1024,256]{1,0:T(8,128)S(1)} %get-tuple-element.10.v2_ref, ...), custom_call_target="tpu_custom_call" | custom-call | tf_op jit(solution)/shard_map/pallas_call | solution.py:356

commit v6 on v5

--- a/solution.py
+++ b/solution.py
@@ -13,12 +13,12 @@
 LOG2E = math.log2(math.e)
 TILE = 256
 LANES = 128
-SIB, LEFT, RIGHT, LEFT_SIB, RIGHT_SIB, OPP, OPP_SIB = range(7)
+SIB, SIDES, SIDES_SIB, OPP, OPP_SIB = range(5)
 
 
 def kernel(n, x0_hbm, v0_hbm, q_hbm, f1_ref, x2_ref, v2_ref, e_ref,
            xs, vs, q_ref, xg, mg, aw, qw, acc, rho, esend, ebuf,
-           load_sem, q_sem, own_send, own_meta_send, fwd_send, fwd_meta_send, recv_sem, meta_recv, e_send, e_recv):
+           load_sem, q_sem, sent, meta_sent, e_sent, meta_recv, e_recv, sib_recv, side_recv, side_sib_recv, opp_recv, opp_sib_recv):
     rows, feat = xs.shape
     tiles = rows // TILE
     per = TILE // LANES
@@ -36,62 +36,59 @@
     def tile_rows(k):
         return pl.ds(k * TILE, TILE) if isinstance(k, int) else pl.ds(pl.multiple_of(k * TILE, TILE), TILE)
 
-    def block_copy(e, k, blk, dev, send, rel):
-        ref = xg.at[e, blk, tile_rows(k), :]
-        return pltpu.make_async_remote_copy(src_ref=ref, dst_ref=ref, send_sem=send, recv_sem=recv_sem.at[rel, e, k],
+    def remote(ref, dev, send, recv):
+        return pltpu.make_async_remote_copy(src_ref=ref, dst_ref=ref, send_sem=send, recv_sem=recv,
                                             device_id={"blk": dev}, device_id_type=MESH)
 
-    def meta_copy(blk, dev, send, rel):
-        ref = mg.at[blk]
-        return pltpu.make_async_remote_copy(src_ref=ref, dst_ref=ref, send_sem=send, recv_sem=meta_recv.at[rel],
-                                            device_id={"blk": dev}, device_id_type=MESH)
+    def block_copy(e, k, blk, dev, recv):
+        return remote(xg.at[e, blk, tile_rows(k), :], dev, sent, recv)
+
+    def meta_copy(blk, dev, rel):
+        return remote(mg.at[blk], dev, meta_sent, meta_recv.at[rel])
 
     def own_copies(e, k):
-        return (block_copy(e, k, me, right, own_send.at[0, e, k], LEFT),
-                block_copy(e, k, me, left, own_send.at[1, e, k], RIGHT),
-                block_copy(e, k, me, sib, own_send.at[2, e, k], SIB))
+        return (block_copy(e, k, me, right, side_recv.at[e, k]),
+                block_copy(e, k, me, left, side_recv.at[e, k]),
+                block_copy(e, k, me, sib, sib_recv.at[e]))
 
     def own_meta():
-        return (meta_copy(me, right, own_meta_send.at[0], LEFT),
-                meta_copy(me, left, own_meta_send.at[1], RIGHT),
-                meta_copy(me, sib, own_meta_send.at[2], SIB))
+        return (meta_copy(me, right, SIDES), meta_copy(me, left, SIDES), meta_copy(me, sib, SIB))
 
     def fwd_left(e, k):
-        return block_copy(e, k, left, sib, fwd_send.at[0, e, k], LEFT_SIB)
+        return block_copy(e, k, left, sib, side_sib_recv.at[e, k])
 
     def fwd_right(e, k):
-        return block_copy(e, k, right, sib, fwd_send.at[1, e, k], RIGHT_SIB)
+        return block_copy(e, k, right, sib, side_sib_recv.at[e, k])
 
     def fwd_opp(e, k):
-        return block_copy(e, k, opp, sib, fwd_send.at[2, e, k], OPP_SIB)
+        return block_copy(e, k, opp, sib, opp_sib_recv.at[e, lax.rem(k, half)])
 
     def pass_right(e, k):
-        return block_copy(e, k, left, right, fwd_send.at[3, e, k], OPP)
+        return block_copy(e, k, left, right, opp_recv.at[e, k])
 
     def pass_left(e, k):
-        return block_copy(e, k, right, left, fwd_send.at[3, e, k], OPP)
+        return block_copy(e, k, right, left, opp_recv.at[e, k - half])
 
     def fwd_meta():
-        return (meta_copy(left, sib, fwd_meta_send.at[0], LEFT_SIB),
-                meta_copy(right, sib, fwd_meta_send.at[1], RIGHT_SIB),
-                meta_copy(left, right, fwd_meta_send.at[2], OPP))
+        return (meta_copy(left, sib, SIDES_SIB), meta_copy(right, sib, SIDES_SIB), meta_copy(left, right, OPP))
 
     def fwd_opp_meta():
-        return meta_copy(opp, sib, fwd_meta_send.at[3], OPP_SIB)
-
-    def arrived(e, k, blk, rel):
-        block_copy(e, k, blk, sib, own_send.at[0, e, k], rel).wait_recv()
-
-    def meta_arrived(blk, rel):
-        meta_copy(blk, sib, own_meta_send.at[0], rel).wait_recv()
+        return meta_copy(opp, sib, OPP_SIB)
+
+    def tiles_arrived(count, recv):
+        remote(xg.at[0, 0, pl.ds(0, count * TILE), :], sib, sent, recv).wait_recv()
+
+    def meta_arrived(count, rel):
+        remote(mg.at[pl.ds(0, count)], sib, meta_sent, meta_recv.at[rel]).wait_recv()
 
     def energy_copy(i):
-        return pltpu.make_async_remote_copy(src_ref=esend, dst_ref=ebuf.at[me], send_sem=e_send.at[i], recv_sem=e_recv.at[i],
+        return pltpu.make_async_remote_copy(src_ref=esend, dst_ref=ebuf.at[me], send_sem=e_sent, recv_sem=e_recv,
                                             device_id={"blk": lax.rem(me + i, n)}, device_id_type=MESH)
 
-    def load(k, which):
+    def load(which, lo, size):
         src, dst = ((x0_hbm, xs), (v0_hbm, vs))[which]
-        return pltpu.make_async_copy(src.at[tile_rows(k), :], dst.at[tile_rows(k), :], load_sem.at[which, k])
+        part = pl.ds(lo, size)
+        return pltpu.make_async_copy(src.at[part, :], dst.at[part, :], load_sem.at[which, 1 if lo else 0])
 
     def pair_tiles(e, pieces, masked=False, finish=None):
         scale = LOG2E / feat
@@ -132,22 +129,26 @@
     barrier = pltpu.get_barrier_semaphore()
     for i in range(1, n):
         pl.semaphore_signal(barrier, inc=1, device_id={"blk": lax.rem(me + i, n)}, device_id_type=MESH)
-    load(0, 0).start()
-    load(0, 1).start()
+    first = [load(which, 0, TILE) for which in range(2)]
+    others = [load(which, TILE, rows - TILE) for which in range(2)]
+    for copy in first:
+        copy.start()
     q_load = pltpu.make_async_copy(q_hbm, q_ref, q_sem)
     rho[...] = jnp.zeros_like(rho)
-    for k in range(1, tiles):
-        load(k, 0).start()
-        load(k, 1).start()
+    for copy in others:
+        copy.start()
     q_load.start()
     acc[...] = jnp.zeros_like(acc)
     for k in range(tiles):
         sl = tile_rows(k)
-        load(k, 0).wait()
-        load(k, 1).wait()
-        x1 = xs[sl, :] + STEP * vs[sl, :]
+        if k < 2:
+            for copy in (first, others)[k]:
+                copy.wait()
+        x0 = xs[sl, :]
+        x1 = x0 + STEP * vs[sl, :]
         xg[1, me, sl, :] = x1.astype(jnp.bfloat16)
-        xg[0, me, sl, :] = xs[sl, :].astype(jnp.bfloat16)
+        xg[0, me, sl, :] = x0.astype(jnp.bfloat16)
+        xs[sl, :] = x1
         if k == 0:
             pl.semaphore_wait(barrier, n - 1)
             for copy in own_copies(1, k):
@@ -178,52 +179,45 @@
     def _(i):
         pair_tiles(1 - i, [(me, k) for k in range(tiles)], masked=True)
 
-    meta_arrived(sib, SIB)
+    meta_arrived(1, SIB)
 
     @pl.loop(0, 2)
     def _(i):
         e = 1 - i
-        for k in range(tiles):
-            arrived(e, k, sib, SIB)
+        tiles_arrived(tiles, sib_recv.at[e])
         pair_tiles(e, [(sib, k) for k in range(tiles)])
 
     def receive_sides(i):
         e, k = 1 - i // tiles, lax.rem(i, tiles)
-        arrived(e, k, left, LEFT)
+        tiles_arrived(2, side_recv.at[e, k])
         fwd_left(e, k).start()
+        fwd_right(e, k).start()
 
         @pl.when(k < half)
         def _():
             pass_right(e, k).start()
 
-        arrived(e, k, right, RIGHT)
-        fwd_right(e, k).start()
-
         @pl.when(k >= half)
         def _():
             pass_left(e, k).start()
 
     def relayed_sides(e, k):
-        arrived(e, k, left_sib, LEFT_SIB)
-        arrived(e, k, right_sib, RIGHT_SIB)
+        tiles_arrived(2, side_sib_recv.at[e, k])
         return [(left_sib, k), (right_sib, k)]
 
     def receive_opposite(e, k):
+        tiles_arrived(2, opp_recv.at[e, k])
         for t in (k, k + half):
-            arrived(e, t, opp, OPP)
             fwd_opp(e, t).start()
 
     def relayed_opposite(e, k):
-        for t in (k, k + half):
-            arrived(e, t, opp_sib, OPP_SIB)
+        tiles_arrived(2, opp_sib_recv.at[e, k])
         return [(opp_sib, k), (opp_sib, k + half)]
 
-    meta_arrived(left, LEFT)
-    meta_arrived(right, RIGHT)
+    meta_arrived(2, SIDES)
     for copy in fwd_meta():
         copy.start()
-    meta_arrived(left_sib, LEFT_SIB)
-    meta_arrived(right_sib, RIGHT_SIB)
+    meta_arrived(2, SIDES_SIB)
 
     @pl.loop(0, 2 * tiles)
     def _(i):
@@ -248,14 +242,14 @@
 
     def last_finish(sl, f0):
         v1 = vs[sl, :] + STEP * f0
-        x2_ref[sl, :] = (xs[sl, :] + STEP * vs[sl, :]) + STEP * v1
+        x2_ref[sl, :] = xs[sl, :] + STEP * v1
         v2_ref[sl, :] = v1 + STEP * f1_ref[sl, :]
 
-    meta_arrived(opp, OPP)
+    meta_arrived(1, OPP)
     fwd_opp_meta().start()
     receive_opposite(1, 0)
     pair_tiles(0, relayed_sides(0, tiles - 1))
-    meta_arrived(opp_sib, OPP_SIB)
+    meta_arrived(1, OPP_SIB)
 
     @pl.loop(0, 2)
     def _(i):
@@ -279,21 +273,12 @@
             pair_tiles(e, [(opp, k), (opp, k + half)] + relayed_opposite(e, k - 1))
 
     pair_tiles(0, relayed_opposite(0, half - 1), finish=last_finish)
-    for i in range(1, n):
-        energy_copy(i).wait_recv()
+    parts = remote(ebuf.at[pl.ds(0, n - 1)], sib, e_sent, e_recv)
+    parts.wait_recv()
     e_ref[...] = ebuf[...]
-
-    for i in range(1, n):
-        energy_copy(i).wait_send()
-    for copy in own_meta() + fwd_meta() + (fwd_opp_meta(),):
-        copy.wait_send()
-
-    @pl.loop(0, 2 * tiles)
-    def _(i):
-        e = 1 - i // tiles
-        k = lax.rem(i, tiles)
-        for copy in own_copies(e, k) + (fwd_left(e, k), fwd_right(e, k), fwd_opp(e, k), pass_right(e, k)):
-            copy.wait_send()
+    parts.wait_send()
+    remote(xg.at[:, pl.ds(0, n - 1)], sib, sent, sib_recv.at[0]).wait_send()
+    remote(mg.at[pl.ds(0, n - 1)], sib, meta_sent, meta_recv.at[0]).wait_send()
 
 
 def write_out(f1_ref, x2_ref, v2_ref, parts_ref, f1_hbm, e_hbm, x2_hbm, v2_hbm, e_ref, sem):
@@ -339,16 +324,18 @@
                 pltpu.VMEM((2, rows, LANES), jnp.float32),
                 pltpu.VMEM((8, LANES), jnp.float32),
                 pltpu.VMEM((n, 8, LANES), jnp.float32),
+                dma((2, 2)),
+                dma,
+                dma,
+                dma,
+                dma,
+                dma((5,)),
+                dma,
+                dma((2,)),
                 dma((2, tiles)),
-                dma,
-                dma((3, 2, tiles)),
-                dma((3,)),
-                dma((4, 2, tiles)),
-                dma((4,)),
-                dma((7, 2, tiles)),
-                dma((7,)),
-                dma((n,)),
-                dma((n,)),
+                dma((2, tiles)),
+                dma((2, tiles // 2)),
+                dma((2, tiles // 2)),
             ],
             compiler_params=pltpu.CompilerParams(collective_id=0, has_side_effects=True, vmem_limit_bytes=52800000),
             cost_estimate=pl.CostEstimate(flops=8 * n * rows * rows * feat, bytes_accessed=20 * rows * feat, transcendentals=2 * n * rows * rows),

time: 47.5 us -> 46.4 us (0.977)
  Pallas kernels: 46.7 us -> 45.5 us
    pallas_call x1, Pallas kernels: 45 us -> 43.8 us  [local_steps(): pl.pallas_call(functools.partial(kernel, n), out_shape=(block, block, blo...]
where the time goes in v6:
time: 46.4 us; the launch traced here: 46.2 us
  Pallas kernels  45.5 us (98%)
  between operations  0.64 us (1%)
    pallas_call x1, Pallas kernels, local_steps(): pl.pallas_call(functools.partial(kernel, n), out_shape=(block, block, blo...  43.8 us
    pallas_call x1, Pallas kernels, local_steps(): pl.pallas_call(write_out, out_shape=(block, jax.ShapeDtypeStruct((1,), jn...  1.71 us

profile of v6, /device:TPU:113, one launch (start us, length us, event | category | flops | bytes accessed | tf_op | source)
XLA Modules:
  0.0 46.2 jit_solution(14455866298677537301)
XLA Ops:
  0.6 43.8 %shard_map.66 = (f32[1024,256]{1,0:T(8,128)S(1)}, f32[1024,256]{1,0:T(8,128)S(1)}, f32[1024,256]{1,0:T(8,128)S(1)}, f32[8,8,128]{2,1,0:T(8,128)S(1)}) custom-call(f32[1024,256]{1,0:T(8,128)} %x0_hbm.1, f32[1024,256]{1,0:T(8,128)} %v0_hbm.1, f32[8,128]{1,0:T(8,128)} %bitcast.1), custom_call_target="tpu_custom_call" | custom-call | flops 17179869184 | bytes 5242880 | tf_op jit(solution)/shard_map/pallas_call | solution.py:310
  44.5 1.7 %shard_map.67 = (f32[1024,256]{1,0:T(8,128)}, f32[1]{0:T(128)}, f32[1024,256]{1,0:T(8,128)}, f32[1024,256]{1,0:T(8,128)}) custom-call(f32[1024,256]{1,0:T(8,128)S(1)} %get-tuple-element.8.f1_ref, f32[1024,256]{1,0:T(8,128)S(1)} %get-tuple-element.9.x2_ref, f32[1024,256]{1,0:T(8,128)S(1)} %get-tuple-element.10.v2_ref, ...), custom_call_target="tpu_custom_call" | custom-call | tf_op jit(solution)/shard_map/pallas_call | solution.py:343

commit v7 on v6

--- a/solution.py
+++ b/solution.py
@@ -23,6 +23,7 @@
     tiles = rows // TILE
     per = TILE // LANES
     half = tiles // 2
+    strips = half * per
     me = lax.axis_index("blk")
     core = lax.rem(me, 2)
     sib = me + 1 - 2 * core
@@ -40,6 +41,21 @@
         return pltpu.make_async_remote_copy(src_ref=ref, dst_ref=ref, send_sem=send, recv_sem=recv,
                                             device_id={"blk": dev}, device_id_type=MESH)
 
+    def strip_rows(r):
+        return pl.ds(r * LANES, LANES) if isinstance(r, int) else pl.ds(pl.multiple_of(r * LANES, LANES), LANES)
+
+    def tile(blk, k):
+        return blk, [k * per + p for p in range(per)]
+
+    def opposite_strips(s):
+        return s, s + strips
+
+    def opposite_piece(blk, s):
+        return blk, opposite_strips(s)
+
+    def strip_copy(e, r, blk, dev, recv):
+        return remote(xg.at[e, blk, strip_rows(r), :], dev, sent, recv)
+
     def block_copy(e, k, blk, dev, recv):
         return remote(xg.at[e, blk, tile_rows(k), :], dev, sent, recv)
 
@@ -60,14 +76,11 @@
     def fwd_right(e, k):
         return block_copy(e, k, right, sib, side_sib_recv.at[e, k])
 
-    def fwd_opp(e, k):
-        return block_copy(e, k, opp, sib, opp_sib_recv.at[e, lax.rem(k, half)])
-
     def pass_right(e, k):
-        return block_copy(e, k, left, right, opp_recv.at[e, k])
+        return [strip_copy(e, k * per + p, left, right, opp_recv.at[e, k * per + p]) for p in range(per)]
 
     def pass_left(e, k):
-        return block_copy(e, k, right, left, opp_recv.at[e, k - half])
+        return [strip_copy(e, k * per + p, right, left, opp_recv.at[e, k * per + p - strips]) for p in range(per)]
 
     def fwd_meta():
         return (meta_copy(left, sib, SIDES_SIB), meta_copy(right, sib, SIDES_SIB), meta_copy(left, right, OPP))
@@ -93,10 +106,10 @@
     def pair_tiles(e, pieces, masked=False, finish=None):
         scale = LOG2E / feat
         cols = []
-        for blk, k in pieces:
-            b_j = xg[e, blk, tile_rows(k), :]
-            a_j = jnp.concatenate([mg[blk, e, pl.ds(k * per + p, 1), :] for p in range(per)], axis=1)
-            q_j = jnp.concatenate([mg[blk, 2, pl.ds(k * per + p, 1), :] for p in range(per)], axis=1)
+        for blk, strips in pieces:
+            b_j = jnp.concatenate([xg[e, blk, strip_rows(r), :] for r in strips], axis=0)
+            a_j = jnp.concatenate([mg[blk, e, pl.ds(r, 1), :] for r in strips], axis=1)
+            q_j = jnp.concatenate([mg[blk, 2, pl.ds(r, 1), :] for r in strips], axis=1)
             cols.append((b_j, a_j, q_j))
         for t in range(tiles):
             sl = tile_rows(t)
@@ -177,7 +190,7 @@
 
     @pl.loop(0, 2)
     def _(i):
-        pair_tiles(1 - i, [(me, k) for k in range(tiles)], masked=True)
+        pair_tiles(1 - i, [tile(me, k) for k in range(tiles)], masked=True)
 
     meta_arrived(1, SIB)
 
@@ -185,7 +198,7 @@
     def _(i):
         e = 1 - i
         tiles_arrived(tiles, sib_recv.at[e])
-        pair_tiles(e, [(sib, k) for k in range(tiles)])
+        pair_tiles(e, [tile(sib, k) for k in range(tiles)])
 
     def receive_sides(i):
         e, k = 1 - i // tiles, lax.rem(i, tiles)
@@ -195,24 +208,26 @@
 
         @pl.when(k < half)
         def _():
-            pass_right(e, k).start()
+            for copy in pass_right(e, k):
+                copy.start()
 
         @pl.when(k >= half)
         def _():
-            pass_left(e, k).start()
+            for copy in pass_left(e, k):
+                copy.start()
 
     def relayed_sides(e, k):
         tiles_arrived(2, side_sib_recv.at[e, k])
-        return [(left_sib, k), (right_sib, k)]
-
-    def receive_opposite(e, k):
-        tiles_arrived(2, opp_recv.at[e, k])
-        for t in (k, k + half):
-            fwd_opp(e, t).start()
-
-    def relayed_opposite(e, k):
-        tiles_arrived(2, opp_sib_recv.at[e, k])
-        return [(opp_sib, k), (opp_sib, k + half)]
+        return [tile(left_sib, k), tile(right_sib, k)]
+
+    def receive_opposite(e, s):
+        tiles_arrived(1, opp_recv.at[e, s])
+        for r in opposite_strips(s):
+            strip_copy(e, r, opp, sib, opp_sib_recv.at[e, s]).start()
+
+    def relayed_opposite(e, s):
+        tiles_arrived(1, opp_sib_recv.at[e, s])
+        return [opposite_piece(opp_sib, s)]
 
     meta_arrived(2, SIDES)
     for copy in fwd_meta():
@@ -223,7 +238,7 @@
     def _(i):
         e, k = 1 - i // tiles, lax.rem(i, tiles)
         receive_sides(i)
-        sides = [(left, k), (right, k)]
+        sides = [tile(left, k), tile(right, k)]
 
         @pl.when(k > 0)
         def _():
@@ -248,8 +263,6 @@
     meta_arrived(1, OPP)
     fwd_opp_meta().start()
     receive_opposite(1, 0)
-    pair_tiles(0, relayed_sides(0, tiles - 1))
-    meta_arrived(1, OPP_SIB)
 
     @pl.loop(0, 2)
     def _(i):
@@ -257,7 +270,8 @@
 
         @pl.when(i == 1)
         def _():
-            pair_tiles(1, relayed_opposite(1, half - 1), finish=first_finish)
+            pair_tiles(1, relayed_opposite(1, strips - 1), finish=first_finish)
+            receive_opposite(0, 0)
             part = jnp.zeros((8, LANES), jnp.float32)
             for r in range(rows // 8):
                 part = part + rho[1, r * 8:(r + 1) * 8, :]
@@ -265,14 +279,20 @@
             ebuf[me] = part
             for p in range(1, n):
                 energy_copy(p).start()
-            receive_opposite(0, 0)
-
-        pair_tiles(e, [(opp, 0), (opp, half)])
-        for k in range(1, half):
-            receive_opposite(e, k)
-            pair_tiles(e, [(opp, k), (opp, k + half)] + relayed_opposite(e, k - 1))
-
-    pair_tiles(0, relayed_opposite(0, half - 1), finish=last_finish)
+
+        pair_tiles(e, [opposite_piece(opp, 0)])
+
+        @pl.when(i == 0)
+        def _():
+            pair_tiles(0, relayed_sides(0, tiles - 1))
+            meta_arrived(1, OPP_SIB)
+
+        @pl.loop(1, strips)
+        def _(s):
+            receive_opposite(e, s)
+            pair_tiles(e, [opposite_piece(opp, s)] + relayed_opposite(e, s - 1))
+
+    pair_tiles(0, relayed_opposite(0, strips - 1), finish=last_finish)
     parts = remote(ebuf.at[pl.ds(0, n - 1)], sib, e_sent, e_recv)
     parts.wait_recv()
     e_ref[...] = ebuf[...]
@@ -334,8 +354,8 @@
                 dma((2,)),
                 dma((2, tiles)),
                 dma((2, tiles)),
-                dma((2, tiles // 2)),
-                dma((2, tiles // 2)),
+                dma((2, rows // (2 * LANES))),
+                dma((2, rows // (2 * LANES))),
             ],
             compiler_params=pltpu.CompilerParams(collective_id=0, has_side_effects=True, vmem_limit_bytes=52800000),
             cost_estimate=pl.CostEstimate(flops=8 * n * rows * rows * feat, bytes_accessed=20 * rows * feat, transcendentals=2 * n * rows * rows),

time: 46.4 us -> 46 us (level)
  no operation moved by 1% of the time
where the time goes in v7:
time: 46 us; the launch traced here: 45.9 us
  Pallas kernels  45.3 us (98%)
  between operations  0.64 us (1%)
    pallas_call x1, Pallas kernels, local_steps(): pl.pallas_call(functools.partial(kernel, n), out_shape=(block, block, blo...  43.6 us
    pallas_call x1, Pallas kernels, local_steps(): pl.pallas_call(write_out, out_shape=(block, jax.ShapeDtypeStruct((1,), jn...  1.71 us

profile of v7, /device:TPU:113, one launch (start us, length us, event | category | flops | bytes accessed | tf_op | source)
XLA Modules:
  0.0 45.9 jit_solution(5735627691438824457)
XLA Ops:
  0.6 43.6 %shard_map.66 = (f32[1024,256]{1,0:T(8,128)S(1)}, f32[1024,256]{1,0:T(8,128)S(1)}, f32[1024,256]{1,0:T(8,128)S(1)}, f32[8,8,128]{2,1,0:T(8,128)S(1)}) custom-call(f32[1024,256]{1,0:T(8,128)} %x0_hbm.1, f32[1024,256]{1,0:T(8,128)} %v0_hbm.1, f32[8,128]{1,0:T(8,128)} %bitcast.1), custom_call_target="tpu_custom_call" | custom-call | flops 17179869184 | bytes 5242880 | tf_op jit(solution)/shard_map/pallas_call | solution.py:330
  44.2 1.7 %shard_map.67 = (f32[1024,256]{1,0:T(8,128)}, f32[1]{0:T(128)}, f32[1024,256]{1,0:T(8,128)}, f32[1024,256]{1,0:T(8,128)}) custom-call(f32[1024,256]{1,0:T(8,128)S(1)} %get-tuple-element.8.f1_ref, f32[1024,256]{1,0:T(8,128)S(1)} %get-tuple-element.9.x2_ref, f32[1024,256]{1,0:T(8,128)S(1)} %get-tuple-element.10.v2_ref, ...), custom_call_target="tpu_custom_call" | custom-call | tf_op jit(solution)/shard_map/pallas_call | solution.py:363

commit v8 on v7

--- a/solution.py
+++ b/solution.py
@@ -83,7 +83,9 @@
         return [strip_copy(e, k * per + p, right, left, opp_recv.at[e, k * per + p - strips]) for p in range(per)]
 
     def fwd_meta():
-        return (meta_copy(left, sib, SIDES_SIB), meta_copy(right, sib, SIDES_SIB), meta_copy(left, right, OPP))
+        return (meta_copy(left, sib, SIDES_SIB), meta_copy(right, sib, SIDES_SIB),
+                remote(mg.at[left, pl.ds(1, 2)], right, meta_sent, meta_recv.at[OPP]),
+                remote(mg.at[right, pl.ds(0, 1)], left, meta_sent, meta_recv.at[OPP]))
 
     def fwd_opp_meta():
         return meta_copy(opp, sib, OPP_SIB)
@@ -268,24 +270,26 @@
     def _(i):
         e = 1 - i
 
+        @pl.when(i == 0)
+        def _():
+            pair_tiles(1, [opposite_piece(opp, 0)])
+            pair_tiles(0, relayed_sides(0, tiles - 1))
+            meta_arrived(1, OPP_SIB)
+
         @pl.when(i == 1)
         def _():
-            pair_tiles(1, relayed_opposite(1, strips - 1), finish=first_finish)
+            relayed = relayed_opposite(1, strips - 1)
             receive_opposite(0, 0)
-            part = jnp.zeros((8, LANES), jnp.float32)
-            for r in range(rows // 8):
-                part = part + rho[1, r * 8:(r + 1) * 8, :]
+            pair_tiles(1, relayed, finish=first_finish)
+            pair_tiles(0, [opposite_piece(opp, 0)])
+            sums = [rho[1, r * 8:(r + 1) * 8, :] for r in range(4)]
+            for r in range(4, rows // 8):
+                sums[r % 4] = sums[r % 4] + rho[1, r * 8:(r + 1) * 8, :]
+            part = (sums[0] + sums[1]) + (sums[2] + sums[3])
             esend[...] = part
             ebuf[me] = part
             for p in range(1, n):
                 energy_copy(p).start()
-
-        pair_tiles(e, [opposite_piece(opp, 0)])
-
-        @pl.when(i == 0)
-        def _():
-            pair_tiles(0, relayed_sides(0, tiles - 1))
-            meta_arrived(1, OPP_SIB)
 
         @pl.loop(1, strips)
         def _(s):

time: 46 us -> 45.9 us (level)
  no operation moved by 1% of the time
where the time goes in v8:
time: 45.9 us; the launch traced here: 45.8 us
  Pallas kernels  45.2 us (98%)
  between operations  0.64 us (1%)
    pallas_call x1, Pallas kernels, local_steps(): pl.pallas_call(functools.partial(kernel, n), out_shape=(block, block, blo...  43.5 us
    pallas_call x1, Pallas kernels, local_steps(): pl.pallas_call(write_out, out_shape=(block, jax.ShapeDtypeStruct((1,), jn...  1.71 us

profile of v8, /device:TPU:113, one launch (start us, length us, event | category | flops | bytes accessed | tf_op | source)
XLA Modules:
  0.0 45.8 jit_solution(13963971786313649261)
XLA Ops:
  0.6 43.5 %shard_map.66 = (f32[1024,256]{1,0:T(8,128)S(1)}, f32[1024,256]{1,0:T(8,128)S(1)}, f32[1024,256]{1,0:T(8,128)S(1)}, f32[8,8,128]{2,1,0:T(8,128)S(1)}) custom-call(f32[1024,256]{1,0:T(8,128)} %x0_hbm.1, f32[1024,256]{1,0:T(8,128)} %v0_hbm.1, f32[8,128]{1,0:T(8,128)} %bitcast.1), custom_call_target="tpu_custom_call" | custom-call | flops 17179869184 | bytes 5242880 | tf_op jit(solution)/shard_map/pallas_call | solution.py:334
  44.1 1.7 %shard_map.67 = (f32[1024,256]{1,0:T(8,128)}, f32[1]{0:T(128)}, f32[1024,256]{1,0:T(8,128)}, f32[1024,256]{1,0:T(8,128)}) custom-call(f32[1024,256]{1,0:T(8,128)S(1)} %get-tuple-element.8.f1_ref, f32[1024,256]{1,0:T(8,128)S(1)} %get-tuple-element.9.x2_ref, f32[1024,256]{1,0:T(8,128)S(1)} %get-tuple-element.10.v2_ref, ...), custom_call_target="tpu_custom_call" | custom-call | tf_op jit(solution)/shard_map/pallas_call | solution.py:367

commit v9 on v8

--- a/solution.py
+++ b/solution.py
@@ -139,7 +139,7 @@
 
     def force(e, sl, rho_t, pull):
         rho_sum = jnp.sum(rho_t, axis=1, keepdims=True)
-        return (rho_sum * xg[e, me, sl, :].astype(jnp.float32) - pull) / feat
+        return (rho_sum * xg[e, me, sl, :].astype(jnp.float32) - pull)
 
     barrier = pltpu.get_barrier_semaphore()
     for i in range(1, n):
@@ -255,10 +255,10 @@
             pair_tiles(e, sides)
 
     def first_finish(sl, f1):
-        f1_ref[sl, :] = f1
+        f1_ref[sl, :] = f1 * (1.0 / feat)
 
     def last_finish(sl, f0):
-        v1 = vs[sl, :] + STEP * f0
+        v1 = vs[sl, :] + (STEP / feat) * f0
         x2_ref[sl, :] = xs[sl, :] + STEP * v1
         v2_ref[sl, :] = v1 + STEP * f1_ref[sl, :]
 

time: 45.9 us -> 45.9 us (level)
  no operation moved by 1% of the time
where the time goes in v9:
time: 45.9 us; the launch traced here: 45.8 us
  Pallas kernels  45.2 us (98%)
  between operations  0.64 us (1%)
    pallas_call x1, Pallas kernels, local_steps(): pl.pallas_call(functools.partial(kernel, n), out_shape=(block, block, blo...  43.4 us
    pallas_call x1, Pallas kernels, local_steps(): pl.pallas_call(write_out, out_shape=(block, jax.ShapeDtypeStruct((1,), jn...  1.71 us

profile of v9, /device:TPU:113, one launch (start us, length us, event | category | flops | bytes accessed | tf_op | source)
XLA Modules:
  0.0 45.8 jit_solution(12766910913574271343)
XLA Ops:
  0.6 43.4 %shard_map.66 = (f32[1024,256]{1,0:T(8,128)S(1)}, f32[1024,256]{1,0:T(8,128)S(1)}, f32[1024,256]{1,0:T(8,128)S(1)}, f32[8,8,128]{2,1,0:T(8,128)S(1)}) custom-call(f32[1024,256]{1,0:T(8,128)} %x0_hbm.1, f32[1024,256]{1,0:T(8,128)} %v0_hbm.1, f32[8,128]{1,0:T(8,128)} %bitcast.1), custom_call_target="tpu_custom_call" | custom-call | flops 17179869184 | bytes 5242880 | tf_op jit(solution)/shard_map/pallas_call | solution.py:334
  44.1 1.7 %shard_map.67 = (f32[1024,256]{1,0:T(8,128)}, f32[1]{0:T(128)}, f32[1024,256]{1,0:T(8,128)}, f32[1024,256]{1,0:T(8,128)}) custom-call(f32[1024,256]{1,0:T(8,128)S(1)} %get-tuple-element.8.f1_ref, f32[1024,256]{1,0:T(8,128)S(1)} %get-tuple-element.9.x2_ref, f32[1024,256]{1,0:T(8,128)S(1)} %get-tuple-element.10.v2_ref, ...), custom_call_target="tpu_custom_call" | custom-call | tf_op jit(solution)/shard_map/pallas_call | solution.py:367
